TPU v7x, 32 devices: a whole 2x2x4 slice. The times are simulated.
32 devices in a mesh: row: 8 (over y, x, core), col: 4 (over z).
Axes of the slice: x: 2, y: 2, z: 4, core: 2. Of those that a mesh axis runs over, the one named last changes fastest.
Arguments:
- features: bfloat16 [16384, 256], P(('row', 'col')), may hold values from -1 to 3
- in_degree: int32 [16384], P(('row', 'col')), may hold values from 512 to 2047
- tile_index: int32 [8192, 2], P(('row', 'col')), may hold values from 0 to 31, as said below
- tile_count: int32 [32], P(('row', 'col')), may hold values from 1 to 256, as said below
- adjacency_tiles: bfloat16 [8192, 128, 128], P(('row', 'col')), may hold values from 0 to 1, as said below
- projection: bfloat16 [512, 256], replicated, may hold values from -0.25 to 0.25
- out_bias: float32 [256], replicated, may hold values from -3 to 3
Outputs:
- hidden_out: bfloat16 [16384, 256], P(('row', 'col'))
Inputs may be any that keep to these rules, and one draw needn't show every extreme that they name: `tile_index`: column 0 is a local row block below 16, column 1 a local column block below 32, in every slot. `tile_count`: slots at or beyond the count hold tiles and indices that must be ignored; some device has all 256 slots live in every draw. `adjacency_tiles`: entries are 0 or 1.
All inputs are finite; a program needn't handle non-finite values.
Results may differ from a plain program's by a relative error of at most 0.0034.
Values may be sent and summed in bfloat16 or wider, within the bound.
A program may use at most 128 MiB of HBM per device.

v0:
```python
import functools

import jax
import jax.numpy as jnp
from jax import lax
from jax.experimental import pallas as pl
from jax.experimental.pallas import tpu as pltpu
from jax.sharding import PartitionSpec as P

BLK = 32
LANES = 128
CHUNKS = 16
DENSE_LIMIT = 24 * 1024 * 1024
MESH = pl.DeviceIdType.MESH


def block_terms(running, col_blocks, index_block, tile_block, live_block):
    picked = col_blocks[index_block[:, 1]]
    kept = jnp.where(live_block[:, None, None], tile_block, jnp.zeros_like(tile_block))
    product = jnp.einsum("kij,kjf->kif", kept, picked, preferred_element_type=jnp.float32)
    flattened = product.reshape(product.shape[0], -1)
    return running.at[index_block[:, 0]].add(flattened)


def local_sparse(features, in_degree, tile_index, tile_count, adjacency_tiles, projection, out_bias):
    feat_width = features.shape[1]
    tile_size = adjacency_tiles.shape[1]
    slot_total = adjacency_tiles.shape[0]
    gathered = lax.all_gather(features, "row", axis=0, tiled=True)
    col_blocks = gathered.reshape(gathered.shape[0] // tile_size, tile_size, feat_width)
    row_blocks = features.shape[0] * lax.axis_size("col") // tile_size
    live_count = tile_count[0]
    zeroed = jnp.zeros((row_blocks, tile_size * feat_width), jnp.float32)

    def one_step(running, offset):
        index_block = lax.dynamic_slice_in_dim(tile_index, offset, BLK, 0)
        tile_block = lax.dynamic_slice_in_dim(adjacency_tiles, offset, BLK, 0)
        live_block = offset + jnp.arange(BLK, dtype=jnp.int32) < live_count
        return (block_terms(running, col_blocks, index_block, tile_block, live_block), None)

    summed, _ = lax.scan(one_step, zeroed, jnp.arange(0, slot_total, BLK, dtype=jnp.int32))
    partial_value = summed.reshape(row_blocks * tile_size, feat_width)
    own_sums = lax.psum_scatter(partial_value, "col", scatter_dimension=0, tiled=True)
    neighbour_mean = (own_sums / in_degree[:, None].astype(jnp.float32)).astype(jnp.bfloat16)
    joined = jnp.concatenate([features, neighbour_mean], axis=1)
    mixed = jnp.dot(joined, projection, preferred_element_type=jnp.float32) + out_bias[None, :]
    return jnp.maximum(mixed, 0.0).astype(jnp.bfloat16)


def densify_kernel(count_ref, place_ref, tiles_ref, dense_ref, stage, sems):
    slots, tile = stage.shape[0], stage.shape[1]
    per = slots // CHUNKS

    def load(i):
        part = pl.ds(i * per, per)
        return pltpu.make_async_copy(tiles_ref.at[part], stage.at[part], sems.at[i])

    for i in range(CHUNKS):
        load(i).start()

    @pl.loop(0, dense_ref.shape[0])
    def _(j):
        dense_ref[j] = jnp.zeros(dense_ref.shape[1:], dense_ref.dtype)

    count = count_ref[0]
    for i in range(CHUNKS):
        load(i).wait()

        @pl.loop(i * per, jnp.minimum((i + 1) * per, jnp.maximum(count, i * per)))
        def _(slot):
            col = place_ref[1, slot]
            row = pl.multiple_of(place_ref[0, slot] * tile, tile)
            dense_ref[col, pl.ds(row, tile), :] += stage[slot]


def fused_kernel(n_row, n_col, feat_ref, dense_ref, degree_ref, proj_ref, bias_ref, out_ref,
                 gathered, acc, hidden, degree_col, send, relayed, landed,
                 ag_send, ag_recv, send_sem, relay_sem, land_sem):
    seg, width = feat_ref.shape
    halves = width // LANES
    blocks = seg // LANES
    chips = n_row // 2
    r = lax.axis_index("row")
    c = lax.axis_index("col")
    sibling = r ^ 1

    barrier = pltpu.get_barrier_semaphore()

    def greet(row, col):
        pl.semaphore_signal(barrier, inc=1, device_id=(row, col), device_id_type=MESH)

    greet(sibling, c)
    for m in range(1, chips):
        greet(r ^ (2 * m), c)

    peers = chips
    for hop in range(1, n_col):
        for step in (-hop, hop):
            inside = (c + step >= 0) & (c + step < n_col)
            peers = peers + jnp.where(inside, 1, 0)

            @pl.when(inside)
            def _():
                greet(r, c + step)

    pl.semaphore_wait(barrier, peers)

    def lanes(h):
        return pl.ds(h * LANES, LANES)

    def gather_copy(h, j):
        if j == 0:
            src, owner, target = feat_ref.at[:, lanes(h)], r, sibling
        elif j < chips:
            src, owner, target = feat_ref.at[:, lanes(h)], r, r ^ (2 * j)
        else:
            owner = r ^ (2 * (j - chips + 1))
            src, target = gathered.at[owner, :, lanes(h)], sibling
        return pltpu.make_async_remote_copy(
            src_ref=src, dst_ref=gathered.at[owner, :, lanes(h)],
            send_sem=ag_send.at[h, j], recv_sem=ag_recv.at[h, j],
            device_id=(target, c), device_id_type=MESH)

    def source(j):
        if j == 0:
            return sibling
        if j < chips:
            return r ^ (2 * j)
        return sibling ^ (2 * (j - chips + 1))

    total = 2 * chips - 1

    def gather_start(h):
        for j in range(1, chips):
            gather_copy(h, j).start()
        gather_copy(h, 0).start()

    gather_start(0)

    def multiply(h, owner, block, first):
        @pl.loop(0, n_col)
        def _(d):
            rows = pl.ds(pl.multiple_of(d * seg, seg), seg)
            left = jnp.concatenate(
                [dense_ref[owner * blocks + k, rows, :] for k in range(blocks)], axis=1)
            product = jnp.dot(left, block, preferred_element_type=jnp.float32)
            if first:
                acc[h, rows, :] = product
            else:
                acc[h, rows, :] += product

    def own_block(h):
        multiply(h, r, feat_ref[:, lanes(h)], True)

    def other_block(h, j):
        gather_copy(h, j).wait_recv()
        if 0 < j < chips:
            gather_copy(h, j + chips - 1).start()
        owner = source(j)
        multiply(h, owner, gathered[owner, :, lanes(h)], False)

    def term(h, d):
        return acc[h, d * seg:(d + 1) * seg, :]

    def relay_copy(h, d, way):
        return pltpu.make_async_remote_copy(
            src_ref=send.at[h, d], dst_ref=relayed.at[h],
            send_sem=send_sem.at[h, d], recv_sem=relay_sem.at[h],
            device_id=(r, c + way), device_id_type=MESH)

    def land_copy(h, d, slot):
        return pltpu.make_async_remote_copy(
            src_ref=send.at[h, d], dst_ref=landed.at[h, slot],
            send_sem=send_sem.at[h, d], recv_sem=land_sem.at[h, slot],
            device_id=(r, d), device_id_type=MESH)

    def routes():
        for d in range(n_col - 1, -1, -1):
            for c_from in range(n_col):
                if c_from != d:
                    yield d, c_from, abs(d - c_from), 1 if d > c_from else -1

    def slot_of(hops, way):
        return hops - 1 + (0 if way > 0 else 2)

    def adds_relay(d, c_from, hops, way):
        return hops == 2 and 0 <= c_from - way < n_col

    def relays(c_from):
        return n_col == 4 and c_from in (0, n_col - 1)

    def send_direct(h, d, hops, way):
        send[h, d] = term(h, d).astype(send.dtype)
        land_copy(h, d, slot_of(hops, way)).start()

    def first_sends(h):
        for d, c_from, hops, way in routes():
            if hops == 3:
                @pl.when(c == c_from)
                def _():
                    send[h, d] = term(h, d).astype(send.dtype)
                    relay_copy(h, d, way).start()
            elif not relays(c_from) and not adds_relay(d, c_from, hops, way):
                @pl.when(c == c_from)
                def _():
                    send_direct(h, d, hops, way)

    def later_sends(h):
        for c_from in range(n_col):
            if relays(c_from):
                @pl.when(c == c_from)
                def _():
                    far = n_col - 1 - c_from
                    way = 1 if far > c_from else -1
                    relay_copy(h, far, way).wait_send()
                    for hops in (2, 1):
                        send_direct(h, c_from + way * hops, hops, way)

    def relay_sends(h):
        for d, c_from, hops, way in routes():
            if adds_relay(d, c_from, hops, way):
                @pl.when(c == c_from)
                def _():
                    relay_copy(h, d, way).wait_recv()
                    send[h, d] = (term(h, d) + relayed[h].astype(jnp.float32)).astype(send.dtype)
                    land_copy(h, d, slot_of(hops, way)).start()

    def finish(h):
        own = pl.ds(pl.multiple_of(c * seg, seg), seg)
        for hops in (1, 2):
            for way in (1, -1):
                origin = c - way * hops

                @pl.when((origin >= 0) & (origin < n_col))
                def _():
                    slot = slot_of(hops, way)
                    land_copy(h, 0, slot).wait_recv()
                    acc[h, own, :] += landed[h, slot].astype(jnp.float32)

        mean = (acc[h, own, :] / degree_col[...]).astype(jnp.bfloat16)
        hidden[...] += jnp.dot(
            mean, proj_ref[width + h * LANES:width + (h + 1) * LANES, :],
            preferred_element_type=jnp.float32)

    for h in range(halves):
        own_block(h)
        if h == 0:
            hidden[...] = jnp.dot(
                feat_ref[...], proj_ref[:width, :],
                preferred_element_type=jnp.float32) + bias_ref[...]
            for b in range(blocks):
                one = degree_ref[b:b + 1, :].astype(jnp.float32)
                degree_col[b * LANES:(b + 1) * LANES, :] = jnp.transpose(
                    jnp.broadcast_to(one, (LANES, LANES)))
        for j in range(total):
            if h > 0 and j == 1:
                later_sends(h - 1)
                relay_sends(h - 1)
            other_block(h, j)
            if j == chips - 1 and h + 1 < halves:
                gather_start(h + 1)
        first_sends(h)
        if h > 0:
            finish(h - 1)
    later_sends(halves - 1)
    relay_sends(halves - 1)
    finish(halves - 1)
    out_ref[...] = jnp.maximum(hidden[...], 0.0).astype(out_ref.dtype)

    for h in range(halves):
        for j in range(total):
            gather_copy(h, j).wait_send()
        for d, c_from, hops, way in routes():
            if hops < 3:
                @pl.when(c == c_from)
                def _():
                    land_copy(h, d, slot_of(hops, way)).wait_send()


def local_dense(n_row, n_col, features, in_degree, tile_index, tile_count, adjacency_tiles, projection, out_bias):
    seg, width = features.shape
    slots, tile, _ = adjacency_tiles.shape
    row_blocks = seg * n_col // tile
    col_blocks = seg * n_row // tile
    halves = width // LANES
    vmem = pl.BlockSpec(memory_space=pltpu.VMEM)
    smem = pl.BlockSpec(memory_space=pltpu.SMEM)
    dense = pl.pallas_call(
        densify_kernel,
        out_shape=pltpu.VMEM((col_blocks, row_blocks * tile, tile), jnp.bfloat16),
        in_specs=[smem, smem, pl.BlockSpec(memory_space=pl.ANY)],
        out_specs=vmem,
        scratch_shapes=[
            pltpu.VMEM((slots, tile, tile), jnp.bfloat16),
            pltpu.SemaphoreType.DMA((CHUNKS,)),
        ],
        compiler_params=pltpu.CompilerParams(vmem_limit_bytes=42 * 1024 * 1024),
    )(tile_count, tile_index.T, adjacency_tiles)
    carry_sem = pltpu.SemaphoreType.DMA((halves, 4))
    gather_sem = pltpu.SemaphoreType.DMA((halves, n_row))
    return pl.pallas_call(
        functools.partial(fused_kernel, n_row, n_col),
        out_shape=jax.ShapeDtypeStruct((seg, projection.shape[1]), jnp.bfloat16),
        in_specs=[vmem] * 5,
        out_specs=vmem,
        scratch_shapes=[
            pltpu.VMEM((n_row, seg, width), jnp.bfloat16),
            pltpu.VMEM((halves, n_col * seg, LANES), jnp.float32),
            pltpu.VMEM((seg, projection.shape[1]), jnp.float32),
            pltpu.VMEM((seg, LANES), jnp.float32),
            pltpu.VMEM((halves, n_col, seg, LANES), jnp.bfloat16),
            pltpu.VMEM((halves, seg, LANES), jnp.bfloat16),
            pltpu.VMEM((halves, 4, seg, LANES), jnp.bfloat16),
            gather_sem, gather_sem,
            carry_sem, pltpu.SemaphoreType.DMA((halves,)), carry_sem,
        ],
        compiler_params=pltpu.CompilerParams(
            collective_id=0, has_side_effects=True, vmem_limit_bytes=24 * 1024 * 1024),
    )(features, dense, in_degree.reshape(seg // LANES, LANES), projection, out_bias[None, :])


def solution(mesh):
    n_row, n_col = mesh.shape["row"], mesh.shape["col"]

    def local(features, in_degree, tile_index, tile_count, adjacency_tiles, projection, out_bias):
        seg, width = features.shape
        slots, tile, _ = adjacency_tiles.shape
        dense_bytes = 2 * seg * n_row * seg * n_col
        fits = (
            dense_bytes <= DENSE_LIMIT and slots <= 256 and slots % CHUNKS == 0
            and tile == LANES and seg % LANES == 0 and width % LANES == 0
            and n_row >= 4 and n_row & (n_row - 1) == 0 and 2 <= n_col <= 4)
        args = (features, in_degree, tile_index, tile_count, adjacency_tiles, projection, out_bias)
        return local_dense(n_row, n_col, *args) if fits else local_sparse(*args)

    return jax.shard_map(
        local,
        mesh=mesh,
        in_specs=(
            P(("row", "col"), None),
            P(("row", "col")),
            P(("row", "col"), None),
            P(("row", "col")),
            P(("row", "col"), None, None),
            P(),
            P(),
        ),
        out_specs=P(("row", "col"), None),
        check_vma=False,
    )
```

profile of v0, /device:TPU:0, one launch (start us, length us, event | category | flops | bytes accessed | tf_op | source)
XLA Modules:
  0.0 47.8 jit_solution(14950645598390619264)
XLA Ops:
  0.0 0.0 copy-start.3
  0.0 0.0 copy-start.1
  0.0 0.0 copy-start.2
  0.0 0.0 copy-start
  0.7 4.2 %shard_map.73.dense_ref = bf16[32,2048,128]{2,1,0:T(8,128)(2,1)S(1)} custom-call(s32[1]{0:T(128)S(6)} %copy.9.count_ref, s32[2,256]{1,0:T(2,128)} %bitcast.5, bf16[256,128,128]{2,1,0:T(8,128)(2,1)} %tiles_ref.1), custom_call_target="tpu_custom_call" | custom-call | tf_op jit(solution)/shard_map/pallas_call | solution.py:288
  4.9 0.0 copy-done.3
  4.9 0.0 copy-done.1
  5.0 0.0 copy-done.2
  5.0 0.0 copy-done
  5.0 42.1 %shard_map.74 = bf16[512,256]{1,0:T(8,128)(2,1)S(1)} custom-call(bf16[512,256]{1,0:T(8,128)(2,1)S(1)} %copy-done, bf16[32,2048,128]{2,1,0:T(8,128)(2,1)S(1)} %shard_map.73.dense_ref, s32[4,128]{1,0:T(4,128)S(1)} %bitcast.3, bf16[512,256]{1,0:T(8,128)(2,1)S(1)} %copy-done.1, f32[1,256]{1,0:T(1,128)S(1)} %bitcast.4), custom_call_target="tpu_custom_call" | custom-call | tf_op jit(solution)/shard_map/pallas_call | solution.py:301
  47.1 0.7 %copy.10 = bf16[512,256]{1,0:T(8,128)(2,1)} copy(bf16[512,256]{1,0:T(8,128)(2,1)S(1)} %shard_map.74) | data formatting | bytes 524288
Async XLA Ops:
  0.0 4.9 %copy-start.3 = (f32[256]{0:T(256)S(1)}, f32[256]{0:T(256)}, u32[]{:S(2)}) copy-start(f32[256]{0:T(256)} %param.13) | copy-start | bytes 3076
  0.0 4.9 %copy-start.1 = (bf16[512,256]{1,0:T(8,128)(2,1)S(1)}, bf16[512,256]{1,0:T(8,128)(2,1)}, u32[]{:S(2)}) copy-start(bf16[512,256]{1,0:T(8,128)(2,1)} %proj_ref.1) | copy-start | bytes 786436
  0.0 4.9 %copy-start.2 = (s32[512]{0:T(512)S(1)}, s32[512]{0:T(512)}, u32[]{:S(2)}) copy-start(s32[512]{0:T(512)} %param.8) | copy-start | bytes 6148
  0.0 5.0 %copy-start = (bf16[512,256]{1,0:T(8,128)(2,1)S(1)}, bf16[512,256]{1,0:T(8,128)(2,1)}, u32[]{:S(2)}) copy-start(bf16[512,256]{1,0:T(8,128)(2,1)} %feat_ref.1) | copy-start | bytes 786436
where the time goes:
time: 48 us; the launch traced here: 47.8 us
  Pallas kernels  46.3 us (96%)
  between operations  0.76 us (2%)
  local copies, waits for them, and re-layouts  0.72 us (2%)
    pallas_call x1, Pallas kernels, local_dense(): pl.pallas_call(functools.partial(fused_kernel, n_row, n_col), out_shape=j...  42.1 us
    pallas_call x1, Pallas kernels, local_dense(): pl.pallas_call(densify_kernel, out_shape=pltpu.VMEM((col_blocks, row_bloc...  4.2 us

commit v1 on v0

v1 whole, which is shorter than its diff:
```python
import functools

import jax
import jax.numpy as jnp
from jax import lax
from jax.experimental import pallas as pl
from jax.experimental.pallas import tpu as pltpu
from jax.sharding import PartitionSpec as P

BLK = 32
LANES = 128
CHUNKS = 16
PIECES = 2
UNROLL = 8
MERGE_LIMIT = 20 * 1024 * 1024
MESH = pl.DeviceIdType.MESH


def block_terms(running, col_blocks, index_block, tile_block, live_block):
    picked = col_blocks[index_block[:, 1]]
    kept = jnp.where(live_block[:, None, None], tile_block, jnp.zeros_like(tile_block))
    product = jnp.einsum("kij,kjf->kif", kept, picked, preferred_element_type=jnp.float32)
    flattened = product.reshape(product.shape[0], -1)
    return running.at[index_block[:, 0]].add(flattened)


def local_sparse(features, in_degree, tile_index, tile_count, adjacency_tiles, projection, out_bias):
    feat_width = features.shape[1]
    tile_size = adjacency_tiles.shape[1]
    slot_total = adjacency_tiles.shape[0]
    gathered = lax.all_gather(features, "row", axis=0, tiled=True)
    col_blocks = gathered.reshape(gathered.shape[0] // tile_size, tile_size, feat_width)
    row_blocks = features.shape[0] * lax.axis_size("col") // tile_size
    live_count = tile_count[0]
    zeroed = jnp.zeros((row_blocks, tile_size * feat_width), jnp.float32)

    def one_step(running, offset):
        index_block = lax.dynamic_slice_in_dim(tile_index, offset, BLK, 0)
        tile_block = lax.dynamic_slice_in_dim(adjacency_tiles, offset, BLK, 0)
        live_block = offset + jnp.arange(BLK, dtype=jnp.int32) < live_count
        return (block_terms(running, col_blocks, index_block, tile_block, live_block), None)

    summed, _ = lax.scan(one_step, zeroed, jnp.arange(0, slot_total, BLK, dtype=jnp.int32))
    partial_value = summed.reshape(row_blocks * tile_size, feat_width)
    own_sums = lax.psum_scatter(partial_value, "col", scatter_dimension=0, tiled=True)
    neighbour_mean = (own_sums / in_degree[:, None].astype(jnp.float32)).astype(jnp.bfloat16)
    joined = jnp.concatenate([features, neighbour_mean], axis=1)
    mixed = jnp.dot(joined, projection, preferred_element_type=jnp.float32) + out_bias[None, :]
    return jnp.maximum(mixed, 0.0).astype(jnp.bfloat16)


def slot_tables(place_ref, count, table_ref, row_blocks, positions):
    slots = place_ref.shape[1]
    chunks = slots // LANES
    slot_row = lax.broadcasted_iota(jnp.int32, (1, slots), 1)
    spot_row = place_ref[1:2, :] * row_blocks + place_ref[0:1, :]
    spot_row = jnp.where(slot_row < count, spot_row, positions)

    def lane(v, i):
        return v[:, i * LANES:(i + 1) * LANES]

    spot = jnp.concatenate(
        [jnp.transpose(jnp.broadcast_to(lane(spot_row, i), (LANES, LANES))) for i in range(chunks)], axis=0)
    slot = lax.broadcasted_iota(jnp.int32, (slots, LANES), 0)
    before = jnp.zeros((slots, LANES), jnp.float32)
    repeat = jnp.zeros((slots, LANES), jnp.float32)
    for i in range(chunks):
        equal = lane(spot_row, i) == spot
        earlier = lane(slot_row, i) < slot
        first = (lane(spot_row, i) < spot) | (equal & earlier)
        before = before + jnp.where(first, 1.0, 0.0)
        repeat = jnp.maximum(repeat, jnp.where(equal & earlier, 1.0, 0.0))
    rank = jnp.sum(before, axis=1, keepdims=True).astype(jnp.int32)
    keep = jnp.max(repeat, axis=1, keepdims=True)
    for i in range(chunks):
        hit = rank == lax.broadcasted_iota(jnp.int32, (slots, LANES), 1) + i * LANES
        order = jnp.sum(jnp.where(hit, slot, 0), axis=0, keepdims=True)
        again = jnp.sum(jnp.where(hit, keep, 0.0), axis=0, keepdims=True)
        table_ref[i:i + 1, :] = order
        table_ref[chunks + i:chunks + i + 1, :] = again.astype(jnp.int32)
    for i in range(positions // LANES):
        here = lax.broadcasted_iota(jnp.int32, (slots, LANES), 1) + i * LANES
        upto = jnp.sum(jnp.where(spot <= here, 1, 0), axis=0, keepdims=True)
        count_here = jnp.sum(jnp.where(spot == here, 1, 0), axis=0, keepdims=True)
        table_ref[2 * chunks + i:2 * chunks + i + 1, :] = jnp.where(count_here > 0, upto - 1, slots)


def fused_kernel(feat_ref, place_ref, count_ref, tiles_ref, degree_ref, proj_ref, bias_ref, out_ref,
                 stage, merged, table_v, table, gathered, acc, hidden, degree_col, send, relayed, landed,
                 tile_sem, table_sem, ag_send, ag_recv, send_sem, relay_sem, land_sem):
    seg, width = feat_ref.shape
    slots, tile, _ = stage.shape
    halves = width // LANES
    blocks = seg // tile
    row_blocks = acc.shape[1] // tile
    positions = blocks * gathered.shape[1] * row_blocks
    half_rows = seg // 2
    piece_rows = seg // PIECES
    per = slots // CHUNKS
    r = lax.axis_index("row")
    c = lax.axis_index("col")
    near = c ^ 1
    upper = c < 2
    outer = (c == 0) | (c == 3)
    dests = (jnp.where(upper, 3, 0), jnp.where(upper, 2, 1), near, c)

    def load(i):
        part = pl.ds(i * per, per)
        return pltpu.make_async_copy(tiles_ref.at[part], stage.at[part], tile_sem.at[i])

    for i in range(CHUNKS):
        load(i).start()

    barrier = pltpu.get_barrier_semaphore()

    def greet(row, col):
        pl.semaphore_signal(barrier, inc=1, device_id=(row, col), device_id_type=MESH)

    for m in (1, 2, 4):
        greet(r ^ m, c)
    greet(r, near)
    greet(r, c ^ 2)

    @pl.when(jnp.logical_not(outer))
    def _():
        greet(r, c ^ 3)

    pl.semaphore_wait(barrier, jnp.where(outer, 5, 6))

    OWN_SIB, OWN_XA, OWN_XB, OWN_YB, OWN_YA, FWD_Y, FWD_X, SIB_X, SIB_Y, SIB_D = range(10)
    first_rows, last_rows = pl.ds(0, half_rows), pl.ds(half_rows, half_rows)
    whole = pl.ds(0, seg)
    gather_plan = {
        OWN_SIB: (0, whole, 1), OWN_XA: (0, first_rows, 2), OWN_XB: (0, last_rows, 2),
        OWN_YB: (0, last_rows, 4), OWN_YA: (0, first_rows, 4),
        FWD_Y: (2, first_rows, 4), FWD_X: (4, last_rows, 2),
        SIB_X: (2, whole, 1), SIB_Y: (4, whole, 1), SIB_D: (6, whole, 1),
    }

    def lanes(h):
        return pl.ds(h * LANES, LANES)

    def gather_copy(h, j):
        flip, rows, step = gather_plan[j]
        owner = r ^ flip
        src = feat_ref.at[rows, lanes(h)] if flip == 0 else gathered.at[h, owner, rows, :]
        return pltpu.make_async_remote_copy(
            src_ref=src, dst_ref=gathered.at[h, owner, rows, :],
            send_sem=ag_send.at[h, j], recv_sem=ag_recv.at[h, j],
            device_id=(r ^ step, c), device_id_type=MESH)

    def gather_own(h):
        for j in (OWN_XA, OWN_YB, OWN_SIB, OWN_XB, OWN_YA):
            gather_copy(h, j).start()

    def forward(h):
        gather_copy(h, OWN_XA).wait_recv()
        gather_copy(h, FWD_Y).start()
        gather_copy(h, OWN_YB).wait_recv()
        gather_copy(h, FWD_X).start()

    def share_near(h):
        gather_copy(h, OWN_XB).wait_recv()
        gather_copy(h, SIB_X).start()
        gather_copy(h, OWN_YA).wait_recv()
        gather_copy(h, SIB_Y).start()

    def share_far(h):
        gather_copy(h, FWD_Y).wait_recv()
        gather_copy(h, FWD_X).wait_recv()
        gather_copy(h, SIB_D).start()

    def block_of(h, flip):
        return feat_ref[:, lanes(h)] if flip == 0 else gathered[h, r ^ flip]

    def product(h, flips, dest):
        columns = []
        for flip in flips:
            base = (r ^ flip) * (blocks * row_blocks)
            line = 2 * (slots // LANES) + base // LANES
            spot = base % LANES + dest * blocks
            columns += [(line, spot + k * row_blocks) for k in range(blocks)]
        left = jnp.concatenate(
            [jnp.concatenate([merged[table[line, spot + b]] for line, spot in columns], axis=1)
             for b in range(blocks)], axis=0)
        right = jnp.concatenate([block_of(h, flip) for flip in flips], axis=0)
        return jnp.dot(left, right, preferred_element_type=jnp.float32)

    def segment(dest):
        return pl.ds(pl.multiple_of(dest * seg, seg), seg)

    def add_pair(h, flips, first):
        @pl.loop(0, 3)
        def _(i):
            dest = jnp.where(i == 0, dests[0], jnp.where(i == 1, dests[1], dests[2]))
            if first:
                acc[h, segment(dest), :] = product(h, flips, dest)
            else:
                acc[h, segment(dest), :] += product(h, flips, dest)

    def piece(q):
        return pl.ds(q * piece_rows, piece_rows)

    def term(h, dest, q):
        return acc[h, pl.ds(pl.multiple_of(dest * seg + q * piece_rows, piece_rows), piece_rows), :]

    def relay_copy(h, i, q):
        return pltpu.make_async_remote_copy(
            src_ref=send.at[h, i, piece(q), :], dst_ref=relayed.at[h, i, piece(q), :],
            send_sem=send_sem.at[h, i, q], recv_sem=relay_sem.at[h, i, q],
            device_id=(r, near), device_id_type=MESH)

    def near_copy(h, q):
        return pltpu.make_async_remote_copy(
            src_ref=send.at[h, 2, piece(q), :], dst_ref=landed.at[h, 0, piece(q), :],
            send_sem=send_sem.at[h, 2, q], recv_sem=land_sem.at[h, 0, q],
            device_id=(r, near), device_id_type=MESH)

    def far_copy(h, i, q):
        return pltpu.make_async_remote_copy(
            src_ref=send.at[h, i, piece(q), :], dst_ref=landed.at[h, 1, piece(q), :],
            send_sem=send_sem.at[h, i, q], recv_sem=land_sem.at[h, 1, q],
            device_id=(r, dests[i]), device_id_type=MESH)

    def send_sum(h, i):
        if i == 2:
            for q in range(PIECES):
                send[h, i, piece(q), :] = term(h, dests[i], q).astype(send.dtype)
                near_copy(h, q).start()
        else:
            @pl.when(outer)
            def _():
                for q in range(PIECES):
                    send[h, i, piece(q), :] = term(h, dests[i], q).astype(send.dtype)
                    relay_copy(h, i, q).start()

    def relay_sum(h, i):
        @pl.when(jnp.logical_not(outer))
        def _():
            for q in range(PIECES):
                relay_copy(h, i, q).wait_recv()
                arrived = relayed[h, i, piece(q), :].astype(jnp.float32)
                send[h, i, piece(q), :] = (term(h, dests[i], q) + arrived).astype(send.dtype)
                far_copy(h, i, q).start()

    def last_pair(h, i):
        acc[h, segment(dests[i]), :] += product(h, (6, 7), dests[i])
        send_sum(h, i)

    def own_segment(h):
        total = product(h, (0, 1), c)
        for flips in ((2, 3), (4, 5), (6, 7)):
            total = total + product(h, flips, c)
        acc[h, segment(c), :] = total

    def finish(h):
        for q in range(PIECES):
            near_copy(h, q).wait_recv()
            far_copy(h, 0, q).wait_recv()
            total = (term(h, c, q) + landed[h, 0, piece(q), :].astype(jnp.float32)
                     + landed[h, 1, piece(q), :].astype(jnp.float32))
            mean = (total / degree_col[piece(q), :]).astype(jnp.bfloat16)
            mixed = hidden[piece(q), :] + jnp.dot(
                mean, proj_ref[width + h * LANES:width + (h + 1) * LANES, :],
                preferred_element_type=jnp.float32)
            if h + 1 < halves:
                hidden[piece(q), :] = mixed
            else:
                out_ref[piece(q), :] = jnp.maximum(mixed, 0.0).astype(out_ref.dtype)

    gather_own(0)
    slot_tables(place_ref, count_ref[0], table_v, row_blocks, positions)
    merged[slots] = jnp.zeros((tile, tile), merged.dtype)
    hidden[...] = jnp.dot(
        feat_ref[...], proj_ref[:width, :], preferred_element_type=jnp.float32) + bias_ref[...]
    for b in range(seg // LANES):
        one = degree_ref[b:b + 1, :].astype(jnp.float32)
        degree_col[b * LANES:(b + 1) * LANES, :] = jnp.transpose(jnp.broadcast_to(one, (LANES, LANES)))
    table_copy = pltpu.make_async_copy(table_v, table, table_sem)
    table_copy.start()
    forward(0)
    gather_own(1)
    table_copy.wait()
    for i in range(CHUNKS):
        load(i).wait()
    running = jnp.zeros((tile, tile), merged.dtype)
    for part in range(slots // LANES):
        def merge(i, running, part=part):
            keep = table[slots // LANES + part, i].astype(jnp.float32)
            kept = jnp.broadcast_to(keep, (16, tile)).astype(running.dtype)
            kept = jnp.concatenate([kept] * (tile // 16), axis=0)
            running = stage[table[part, i]] + running * kept
            merged[part * LANES + i] = running
            return running
        running = lax.fori_loop(0, LANES, merge, running, unroll=UNROLL)

    share_near(0)
    gather_copy(0, OWN_SIB).wait_recv()
    add_pair(0, (0, 1), True)
    gather_copy(0, SIB_X).wait_recv()
    add_pair(0, (2, 3), False)
    share_far(0)
    gather_copy(0, SIB_Y).wait_recv()
    add_pair(0, (4, 5), False)
    gather_copy(0, SIB_D).wait_recv()
    last_pair(0, 0)
    forward(1)
    last_pair(0, 1)
    last_pair(0, 2)
    share_near(1)
    own_segment(0)
    gather_copy(1, OWN_SIB).wait_recv()
    add_pair(1, (0, 1), True)
    share_far(1)
    gather_copy(1, SIB_X).wait_recv()
    add_pair(1, (2, 3), False)
    gather_copy(1, SIB_Y).wait_recv()
    add_pair(1, (4, 5), False)
    relay_sum(0, 0)
    gather_copy(1, SIB_D).wait_recv()
    for i in range(3):
        last_pair(1, i)
    relay_sum(0, 1)
    own_segment(1)
    finish(0)
    relay_sum(1, 0)
    relay_sum(1, 1)
    finish(1)

    for h in range(halves):
        for j in range(10):
            gather_copy(h, j).wait_send()
        for q in range(PIECES):
            for i in range(2):
                relay_copy(h, i, q).wait_send()
            near_copy(h, q).wait_send()


def local_fused(n_row, n_col, features, in_degree, tile_index, tile_count, adjacency_tiles, projection, out_bias):
    seg, width = features.shape
    slots, tile, _ = adjacency_tiles.shape
    halves = width // LANES
    positions = (seg * n_col // tile) * (seg * n_row // tile)
    lines = 2 * (slots // LANES) + positions // LANES
    vmem = pl.BlockSpec(memory_space=pltpu.VMEM)
    smem = pl.BlockSpec(memory_space=pltpu.SMEM)
    gather_sem = pltpu.SemaphoreType.DMA((halves, 10))
    return pl.pallas_call(
        fused_kernel,
        out_shape=jax.ShapeDtypeStruct((seg, projection.shape[1]), jnp.bfloat16),
        in_specs=[vmem, vmem, smem, pl.BlockSpec(memory_space=pl.ANY), vmem, vmem, vmem],
        out_specs=vmem,
        scratch_shapes=[
            pltpu.VMEM((slots, tile, tile), jnp.bfloat16),
            pltpu.VMEM((slots + 1, tile, tile), jnp.bfloat16),
            pltpu.VMEM((lines, LANES), jnp.int32),
            pltpu.SMEM((lines, LANES), jnp.int32),
            pltpu.VMEM((halves, n_row, seg, LANES), jnp.bfloat16),
            pltpu.VMEM((halves, n_col * seg, LANES), jnp.float32),
            pltpu.VMEM((seg, projection.shape[1]), jnp.float32),
            pltpu.VMEM((seg, LANES), jnp.float32),
            pltpu.VMEM((halves, 3, seg, LANES), jnp.bfloat16),
            pltpu.VMEM((halves, 2, seg, LANES), jnp.bfloat16),
            pltpu.VMEM((halves, 2, seg, LANES), jnp.bfloat16),
            pltpu.SemaphoreType.DMA((CHUNKS,)),
            pltpu.SemaphoreType.DMA,
            gather_sem, gather_sem,
            pltpu.SemaphoreType.DMA((halves, 3, PIECES)),
            pltpu.SemaphoreType.DMA((halves, 2, PIECES)),
            pltpu.SemaphoreType.DMA((halves, 2, PIECES)),
        ],
        compiler_params=pltpu.CompilerParams(
            collective_id=0, has_side_effects=True, vmem_limit_bytes=56 * 1024 * 1024),
    )(features, tile_index.T, tile_count, adjacency_tiles,
      in_degree.reshape(seg // LANES, LANES), projection, out_bias[None, :])


def solution(mesh):
    n_row, n_col = mesh.shape["row"], mesh.shape["col"]

    def local(features, in_degree, tile_index, tile_count, adjacency_tiles, projection, out_bias):
        seg, width = features.shape
        slots, tile, _ = adjacency_tiles.shape
        positions = (seg * n_col // LANES) * (seg * n_row // LANES)
        fits = (
            n_row == 8 and n_col == 4 and tile == LANES and slots <= 256 and slots % LANES == 0
            and 4 * slots * tile * tile <= MERGE_LIMIT
            and seg % (2 * LANES) == 0 and width == 2 * LANES and positions % LANES == 0
            and LANES % (positions // n_row) == 0)
        args = (features, in_degree, tile_index, tile_count, adjacency_tiles, projection, out_bias)
        return local_fused(n_row, n_col, *args) if fits else local_sparse(*args)

    return jax.shard_map(
        local,
        mesh=mesh,
        in_specs=(
            P(("row", "col"), None),
            P(("row", "col")),
            P(("row", "col"), None),
            P(("row", "col")),
            P(("row", "col"), None, None),
            P(),
            P(),
        ),
        out_specs=P(("row", "col"), None),
        check_vma=False,
    )
```

time: 48 us -> 41.6 us (0.87)
  Pallas kernels: 46.3 us -> 39.1 us
  local copies, waits for them, and re-layouts: 0.72 us -> 1.67 us
    pallas_call x2 -> x1, Pallas kernels: 46.3 us -> 39.1 us  [local_fused(): pl.pallas_call(fused_kernel, out_shape=jax.ShapeDtypeStruct((seg, project...]
    unnamed x9 -> x1, local copies, waits for them, and re-layouts: 0.72 us -> 1.67 us
where the time goes in v1:
time: 41.6 us; the launch traced here: 41.4 us
  Pallas kernels  39.1 us (94%)
  local copies, waits for them, and re-layouts  1.67 us (4%)
  between operations  0.66 us (2%)
    pallas_call x1, Pallas kernels, local_fused(): pl.pallas_call(fused_kernel, out_shape=jax.ShapeDtypeStruct((seg, project...  39.1 us
    unnamed x1, local copies, waits for them, and re-layouts  1.67 us

profile of v1, /device:TPU:0, one launch (start us, length us, event | category | flops | bytes accessed | tf_op | source)
XLA Modules:
  0.0 41.4 jit_solution(15442475745358289607)
XLA Ops:
  0.7 39.1 %shard_map.73 = bf16[512,256]{1,0:T(8,128)(2,1)} custom-call(bf16[512,256]{1,0:T(8,128)(2,1)} %feat_ref.1, s32[2,256]{1,0:T(2,128)} %bitcast.3, s32[1]{0:T(128)S(6)} %copy.9.count_ref, bf16[256,128,128]{2,1,0:T(8,128)(2,1)} %tiles_ref.1, s32[4,128]{1,0:T(4,128)} %bitcast.4, bf16[512,256]{1,0:T(8,128)(2,1)} %proj_ref.1, f32[1,256]{1,0:T(1,128)} %bitcast.5), custom_call_target="tpu_custom_call" | custom-call | tf_op jit(solution)/shard_map/pallas_call | solution.py:348
  39.7 1.7 %copy.10 = bf16[512,256]{1,0:T(8,128)(2,1)} copy(bf16[512,256]{1,0:T(8,128)(2,1)} %shard_map.73) | data formatting | bytes 524288

commit v2 on v1

--- a/solution.py
+++ b/solution.py
@@ -11,6 +11,7 @@
 LANES = 128
 CHUNKS = 16
 PIECES = 2
+NEAR = 4
 UNROLL = 8
 MERGE_LIMIT = 20 * 1024 * 1024
 MESH = pl.DeviceIdType.MESH
@@ -85,17 +86,20 @@
         table_ref[2 * chunks + i:2 * chunks + i + 1, :] = jnp.where(count_here > 0, upto - 1, slots)
 
 
-def fused_kernel(feat_ref, place_ref, count_ref, tiles_ref, degree_ref, proj_ref, bias_ref, out_ref,
-                 stage, merged, table_v, table, gathered, acc, hidden, degree_col, send, relayed, landed,
-                 tile_sem, table_sem, ag_send, ag_recv, send_sem, relay_sem, land_sem):
+def fused_kernel(feat_hbm, place_hbm, count_ref, tiles_ref, degree_hbm, proj_hbm, bias_hbm, out_ref,
+                 feat_ref, place_ref, degree_ref, proj_ref, bias_ref,
+                 stage, merged, table_v, table, gathered, acc, own, hidden, degree_col,
+                 send, send_near, relayed, far, near_in,
+                 in_sem, tile_sem, table_sem, ag_send, ag_recv,
+                 send_sem, relay_sem, far_sem, near_send, near_recv):
     seg, width = feat_ref.shape
     slots, tile, _ = stage.shape
     halves = width // LANES
     blocks = seg // tile
-    row_blocks = acc.shape[1] // tile
-    positions = blocks * gathered.shape[1] * row_blocks
+    n_row, n_col = gathered.shape[1], 4
+    row_blocks = n_col * blocks
+    positions = blocks * n_row * row_blocks
     half_rows = seg // 2
-    piece_rows = seg // PIECES
     per = slots // CHUNKS
     r = lax.axis_index("row")
     c = lax.axis_index("col")
@@ -104,12 +108,18 @@
     outer = (c == 0) | (c == 3)
     dests = (jnp.where(upper, 3, 0), jnp.where(upper, 2, 1), near, c)
 
+    inputs = [(place_hbm, place_ref), (feat_hbm, feat_ref),
+              (degree_hbm, degree_ref), (proj_hbm, proj_ref), (bias_hbm, bias_ref)]
+
+    def fetch(i):
+        return pltpu.make_async_copy(*inputs[i], in_sem.at[i])
+
     def load(i):
         part = pl.ds(i * per, per)
         return pltpu.make_async_copy(tiles_ref.at[part], stage.at[part], tile_sem.at[i])
 
-    for i in range(CHUNKS):
-        load(i).start()
+    for i in range(2):
+        fetch(i).start()
 
     barrier = pltpu.get_barrier_semaphore()
 
@@ -125,7 +135,10 @@
     def _():
         greet(r, c ^ 3)
 
-    pl.semaphore_wait(barrier, jnp.where(outer, 5, 6))
+    for i in range(CHUNKS):
+        load(i).start()
+    for i in range(2, len(inputs)):
+        fetch(i).start()
 
     OWN_SIB, OWN_XA, OWN_XB, OWN_YB, OWN_YA, FWD_Y, FWD_X, SIB_X, SIB_Y, SIB_D = range(10)
     first_rows, last_rows = pl.ds(0, half_rows), pl.ds(half_rows, half_rows)
@@ -170,7 +183,12 @@
         gather_copy(h, FWD_X).wait_recv()
         gather_copy(h, SIB_D).start()
 
+    def wait_for(h, j):
+        gather_copy(h, j).wait_recv()
+
     def block_of(h, flip):
+        if h is None:
+            return jnp.concatenate([block_of(i, flip) for i in range(halves)], axis=1)
         return feat_ref[:, lanes(h)] if flip == 0 else gathered[h, r ^ flip]
 
     def product(h, flips, dest):
@@ -186,154 +204,172 @@
         right = jnp.concatenate([block_of(h, flip) for flip in flips], axis=0)
         return jnp.dot(left, right, preferred_element_type=jnp.float32)
 
-    def segment(dest):
-        return pl.ds(pl.multiple_of(dest * seg, seg), seg)
-
-    def add_pair(h, flips, first):
-        @pl.loop(0, 3)
+    def add_pair(h, flips, count, first):
+        @pl.loop(0, count)
         def _(i):
-            dest = jnp.where(i == 0, dests[0], jnp.where(i == 1, dests[1], dests[2]))
+            dest = jnp.where(i == 0, dests[0], dests[1])
             if first:
-                acc[h, segment(dest), :] = product(h, flips, dest)
+                acc[h, i] = product(h, flips, dest)
             else:
-                acc[h, segment(dest), :] += product(h, flips, dest)
-
-    def piece(q):
-        return pl.ds(q * piece_rows, piece_rows)
-
-    def term(h, dest, q):
-        return acc[h, pl.ds(pl.multiple_of(dest * seg + q * piece_rows, piece_rows), piece_rows), :]
+                acc[h, i] += product(h, flips, dest)
+
+    def piece(q, pieces):
+        return pl.ds(q * (seg // pieces), seg // pieces)
 
     def relay_copy(h, i, q):
+        rows = piece(q, PIECES)
         return pltpu.make_async_remote_copy(
-            src_ref=send.at[h, i, piece(q), :], dst_ref=relayed.at[h, i, piece(q), :],
+            src_ref=send.at[h, i, rows, :], dst_ref=relayed.at[h, i, rows, :],
             send_sem=send_sem.at[h, i, q], recv_sem=relay_sem.at[h, i, q],
             device_id=(r, near), device_id_type=MESH)
 
-    def near_copy(h, q):
+    def far_copy(h, i, q):
+        rows = piece(q, PIECES)
         return pltpu.make_async_remote_copy(
-            src_ref=send.at[h, 2, piece(q), :], dst_ref=landed.at[h, 0, piece(q), :],
-            send_sem=send_sem.at[h, 2, q], recv_sem=land_sem.at[h, 0, q],
+            src_ref=send.at[h, i, rows, :], dst_ref=far.at[h, rows, :],
+            send_sem=send_sem.at[h, i, q], recv_sem=far_sem.at[h, q],
+            device_id=(r, dests[i]), device_id_type=MESH)
+
+    def near_copy(q):
+        rows = piece(q, NEAR)
+        return pltpu.make_async_remote_copy(
+            src_ref=send_near.at[rows, :], dst_ref=near_in.at[rows, :],
+            send_sem=near_send.at[q], recv_sem=near_recv.at[q],
             device_id=(r, near), device_id_type=MESH)
 
-    def far_copy(h, i, q):
-        return pltpu.make_async_remote_copy(
-            src_ref=send.at[h, i, piece(q), :], dst_ref=landed.at[h, 1, piece(q), :],
-            send_sem=send_sem.at[h, i, q], recv_sem=land_sem.at[h, 1, q],
-            device_id=(r, dests[i]), device_id_type=MESH)
-
-    def send_sum(h, i):
-        if i == 2:
+    def last_pair(h, i):
+        acc[h, i] += product(h, (6, 7), dests[i])
+
+        @pl.when(outer)
+        def _():
             for q in range(PIECES):
-                send[h, i, piece(q), :] = term(h, dests[i], q).astype(send.dtype)
-                near_copy(h, q).start()
-        else:
-            @pl.when(outer)
-            def _():
-                for q in range(PIECES):
-                    send[h, i, piece(q), :] = term(h, dests[i], q).astype(send.dtype)
-                    relay_copy(h, i, q).start()
-
-    def relay_sum(h, i):
+                rows = piece(q, PIECES)
+                send[h, i, rows, :] = acc[h, i, rows, :].astype(send.dtype)
+                relay_copy(h, i, q).start()
+
+    def relay_sum(h, i, q):
         @pl.when(jnp.logical_not(outer))
         def _():
-            for q in range(PIECES):
-                relay_copy(h, i, q).wait_recv()
-                arrived = relayed[h, i, piece(q), :].astype(jnp.float32)
-                send[h, i, piece(q), :] = (term(h, dests[i], q) + arrived).astype(send.dtype)
-                far_copy(h, i, q).start()
-
-    def last_pair(h, i):
-        acc[h, segment(dests[i]), :] += product(h, (6, 7), dests[i])
-        send_sum(h, i)
-
-    def own_segment(h):
-        total = product(h, (0, 1), c)
-        for flips in ((2, 3), (4, 5), (6, 7)):
-            total = total + product(h, flips, c)
-        acc[h, segment(c), :] = total
-
-    def finish(h):
-        for q in range(PIECES):
-            near_copy(h, q).wait_recv()
-            far_copy(h, 0, q).wait_recv()
-            total = (term(h, c, q) + landed[h, 0, piece(q), :].astype(jnp.float32)
-                     + landed[h, 1, piece(q), :].astype(jnp.float32))
-            mean = (total / degree_col[piece(q), :]).astype(jnp.bfloat16)
-            mixed = hidden[piece(q), :] + jnp.dot(
-                mean, proj_ref[width + h * LANES:width + (h + 1) * LANES, :],
-                preferred_element_type=jnp.float32)
-            if h + 1 < halves:
-                hidden[piece(q), :] = mixed
-            else:
-                out_ref[piece(q), :] = jnp.maximum(mixed, 0.0).astype(out_ref.dtype)
-
-    gather_own(0)
-    slot_tables(place_ref, count_ref[0], table_v, row_blocks, positions)
-    merged[slots] = jnp.zeros((tile, tile), merged.dtype)
-    hidden[...] = jnp.dot(
-        feat_ref[...], proj_ref[:width, :], preferred_element_type=jnp.float32) + bias_ref[...]
-    for b in range(seg // LANES):
-        one = degree_ref[b:b + 1, :].astype(jnp.float32)
-        degree_col[b * LANES:(b + 1) * LANES, :] = jnp.transpose(jnp.broadcast_to(one, (LANES, LANES)))
+            rows = piece(q, PIECES)
+            relay_copy(h, i, q).wait_recv()
+            total = acc[h, i, rows, :] + relayed[h, i, rows, :].astype(jnp.float32)
+            send[h, i, rows, :] = total.astype(send.dtype)
+            far_copy(h, i, q).start()
+
+    def near_segment():
+        send_near[...] = product(None, range(n_row), near).astype(send_near.dtype)
+        for q in range(NEAR):
+            near_copy(q).start()
+
+    def own_segment():
+        own[...] = product(None, range(n_row), c)
+
+    def finish():
+        for q in range(NEAR):
+            rows = piece(q, NEAR)
+            if q % (NEAR // PIECES) == 0:
+                for h in range(halves):
+                    far_copy(h, 0, q // (NEAR // PIECES)).wait_recv()
+            near_copy(q).wait_recv()
+            divisor = degree_col[rows, :]
+            mean = jnp.concatenate(
+                [((own[rows, lanes(h)] + far[h, rows, :].astype(jnp.float32)
+                   + near_in[rows, lanes(h)].astype(jnp.float32)) / divisor).astype(jnp.bfloat16)
+                 for h in range(halves)], axis=1)
+            mixed = hidden[rows, :] + jnp.dot(
+                mean, proj_ref[width:, :], preferred_element_type=jnp.float32)
+            out_ref[rows, :] = jnp.maximum(mixed, 0.0).astype(out_ref.dtype)
+
+    def tables():
+        fetch(0).wait()
+        slot_tables(place_ref, count_ref[0], table_v, row_blocks, positions)
+
     table_copy = pltpu.make_async_copy(table_v, table, table_sem)
-    table_copy.start()
-    forward(0)
-    gather_own(1)
-    table_copy.wait()
-    for i in range(CHUNKS):
-        load(i).wait()
-    running = jnp.zeros((tile, tile), merged.dtype)
-    for part in range(slots // LANES):
-        def merge(i, running, part=part):
+
+    def prepare():
+        merged[slots] = jnp.zeros((tile, tile), merged.dtype)
+        for i in range(2, len(inputs)):
+            fetch(i).wait()
+        hidden[...] = jnp.dot(
+            feat_ref[...], proj_ref[:width, :], preferred_element_type=jnp.float32) + bias_ref[...]
+        for b in range(seg // LANES):
+            one = degree_ref[b:b + 1, :].astype(jnp.float32)
+            degree_col[b * LANES:(b + 1) * LANES, :] = jnp.transpose(jnp.broadcast_to(one, (LANES, LANES)))
+
+    def merge_slots(part, running):
+        def merge(i, running):
             keep = table[slots // LANES + part, i].astype(jnp.float32)
             kept = jnp.broadcast_to(keep, (16, tile)).astype(running.dtype)
             kept = jnp.concatenate([kept] * (tile // 16), axis=0)
             running = stage[table[part, i]] + running * kept
             merged[part * LANES + i] = running
             return running
-        running = lax.fori_loop(0, LANES, merge, running, unroll=UNROLL)
-
-    share_near(0)
-    gather_copy(0, OWN_SIB).wait_recv()
-    add_pair(0, (0, 1), True)
-    gather_copy(0, SIB_X).wait_recv()
-    add_pair(0, (2, 3), False)
-    share_far(0)
-    gather_copy(0, SIB_Y).wait_recv()
-    add_pair(0, (4, 5), False)
-    gather_copy(0, SIB_D).wait_recv()
-    last_pair(0, 0)
-    forward(1)
-    last_pair(0, 1)
-    last_pair(0, 2)
-    share_near(1)
-    own_segment(0)
-    gather_copy(1, OWN_SIB).wait_recv()
-    add_pair(1, (0, 1), True)
-    share_far(1)
-    gather_copy(1, SIB_X).wait_recv()
-    add_pair(1, (2, 3), False)
-    gather_copy(1, SIB_Y).wait_recv()
-    add_pair(1, (4, 5), False)
-    relay_sum(0, 0)
-    gather_copy(1, SIB_D).wait_recv()
-    for i in range(3):
-        last_pair(1, i)
-    relay_sum(0, 1)
-    own_segment(1)
-    finish(0)
-    relay_sum(1, 0)
-    relay_sum(1, 1)
-    finish(1)
+        return lax.fori_loop(0, LANES, merge, running, unroll=UNROLL)
+
+    def wait_loads():
+        table_copy.wait()
+        for i in range(CHUNKS):
+            load(i).wait()
+
+    def step(name, run, *args):
+        with jax.named_scope(name):
+            return run(*args)
+
+    step("tables", tables)
+    step("w_feat", fetch(1).wait)
+    step("barrier", pl.semaphore_wait, barrier, jnp.where(outer, 5, 6))
+    step("own0", gather_own, 0)
+    table_copy.start()
+    step("prepare", prepare)
+    step("loads", wait_loads)
+    running = step("merge0", merge_slots, 0, jnp.zeros((tile, tile), merged.dtype))
+    step("forward0", forward, 0)
+    step("own1", gather_own, 1)
+    for part in range(1, slots // LANES):
+        running = step("merge1", merge_slots, part, running)
+    step("share_near0", share_near, 0)
+    step("w_sib0", wait_for, 0, OWN_SIB)
+    step("pair0a", add_pair, 0, (0, 1), 2, True)
+    step("w_x0", wait_for, 0, SIB_X)
+    step("pair0x", add_pair, 0, (2, 3), 2, False)
+    step("share_far0", share_far, 0)
+    step("w_y0", wait_for, 0, SIB_Y)
+    step("pair0y", add_pair, 0, (4, 5), 2, False)
+    step("w_d0", wait_for, 0, SIB_D)
+    step("last00", last_pair, 0, 0)
+    step("forward1", forward, 1)
+    step("last01", last_pair, 0, 1)
+    step("w_sib1", wait_for, 1, OWN_SIB)
+    step("pair1a", add_pair, 1, (0, 1), 2, True)
+    step("share_near1", share_near, 1)
+    step("relay000", relay_sum, 0, 0, 0)
+    step("w_x1", wait_for, 1, SIB_X)
+    step("pair1x", add_pair, 1, (2, 3), 2, False)
+    step("share_far1", share_far, 1)
+    step("w_y1", wait_for, 1, SIB_Y)
+    step("pair1y", add_pair, 1, (4, 5), 2, False)
+    step("relay001", relay_sum, 0, 0, 1)
+    step("w_d1", wait_for, 1, SIB_D)
+    step("last10", last_pair, 1, 0)
+    step("last11", last_pair, 1, 1)
+    step("relay010", relay_sum, 0, 1, 0)
+    step("near_seg", near_segment)
+    step("relay011", relay_sum, 0, 1, 1)
+    step("relay100", relay_sum, 1, 0, 0)
+    step("own_seg", own_segment)
+    step("relay101", relay_sum, 1, 0, 1)
+    step("relay110", relay_sum, 1, 1, 0)
+    step("relay111", relay_sum, 1, 1, 1)
+    step("finish", finish)
 
     for h in range(halves):
         for j in range(10):
             gather_copy(h, j).wait_send()
-        for q in range(PIECES):
-            for i in range(2):
+        for i in range(2):
+            for q in range(PIECES):
                 relay_copy(h, i, q).wait_send()
-            near_copy(h, q).wait_send()
+    for q in range(NEAR):
+        near_copy(q).wait_send()
 
 
 def local_fused(n_row, n_col, features, in_degree, tile_index, tile_count, adjacency_tiles, projection, out_bias):
@@ -342,37 +378,50 @@
     halves = width // LANES
     positions = (seg * n_col // tile) * (seg * n_row // tile)
     lines = 2 * (slots // LANES) + positions // LANES
-    vmem = pl.BlockSpec(memory_space=pltpu.VMEM)
-    smem = pl.BlockSpec(memory_space=pltpu.SMEM)
+    hbm = pl.BlockSpec(memory_space=pltpu.HBM)
     gather_sem = pltpu.SemaphoreType.DMA((halves, 10))
+    relay_sem = pltpu.SemaphoreType.DMA((halves, 2, PIECES))
+    near_sem = pltpu.SemaphoreType.DMA((NEAR,))
+    args = [features, tile_index.T, tile_count, adjacency_tiles,
+            in_degree.reshape(seg // LANES, LANES), projection, out_bias[None, :]]
+    specs = [hbm] * len(args)
+    specs[2] = pl.BlockSpec(memory_space=pltpu.SMEM)
+    args = [a if i == 2 else pltpu.with_memory_space_constraint(a, pltpu.HBM) for i, a in enumerate(args)]
     return pl.pallas_call(
         fused_kernel,
         out_shape=jax.ShapeDtypeStruct((seg, projection.shape[1]), jnp.bfloat16),
-        in_specs=[vmem, vmem, smem, pl.BlockSpec(memory_space=pl.ANY), vmem, vmem, vmem],
-        out_specs=vmem,
+        in_specs=specs,
+        out_specs=pl.BlockSpec(memory_space=pltpu.VMEM),
         scratch_shapes=[
+            pltpu.VMEM(features.shape, features.dtype),
+            pltpu.VMEM((2, slots), jnp.int32),
+            pltpu.VMEM((seg // LANES, LANES), jnp.int32),
+            pltpu.VMEM(projection.shape, projection.dtype),
+            pltpu.VMEM((1, projection.shape[1]), jnp.float32),
             pltpu.VMEM((slots, tile, tile), jnp.bfloat16),
             pltpu.VMEM((slots + 1, tile, tile), jnp.bfloat16),
             pltpu.VMEM((lines, LANES), jnp.int32),
             pltpu.SMEM((lines, LANES), jnp.int32),
             pltpu.VMEM((halves, n_row, seg, LANES), jnp.bfloat16),
-            pltpu.VMEM((halves, n_col * seg, LANES), jnp.float32),
+            pltpu.VMEM((halves, 2, seg, LANES), jnp.float32),
+            pltpu.VMEM((seg, width), jnp.float32),
             pltpu.VMEM((seg, projection.shape[1]), jnp.float32),
             pltpu.VMEM((seg, LANES), jnp.float32),
-            pltpu.VMEM((halves, 3, seg, LANES), jnp.bfloat16),
             pltpu.VMEM((halves, 2, seg, LANES), jnp.bfloat16),
+            pltpu.VMEM((seg, width), jnp.bfloat16),
             pltpu.VMEM((halves, 2, seg, LANES), jnp.bfloat16),
+            pltpu.VMEM((halves, seg, LANES), jnp.bfloat16),
+            pltpu.VMEM((seg, width), jnp.bfloat16),
+            pltpu.SemaphoreType.DMA((len(args) - 2,)),
             pltpu.SemaphoreType.DMA((CHUNKS,)),
             pltpu.SemaphoreType.DMA,
             gather_sem, gather_sem,
-            pltpu.SemaphoreType.DMA((halves, 3, PIECES)),
-            pltpu.SemaphoreType.DMA((halves, 2, PIECES)),
-            pltpu.SemaphoreType.DMA((halves, 2, PIECES)),
+            relay_sem, relay_sem, pltpu.SemaphoreType.DMA((halves, PIECES)),
+            near_sem, near_sem,
         ],
         compiler_params=pltpu.CompilerParams(
-            collective_id=0, has_side_effects=True, vmem_limit_bytes=56 * 1024 * 1024),
-    )(features, tile_index.T, tile_count, adjacency_tiles,
-      in_degree.reshape(seg // LANES, LANES), projection, out_bias[None, :])
+            collective_id=0, has_side_effects=True, vmem_limit_bytes=48 * 1024 * 1024),
+    )(*args)
 
 
 def solution(mesh):

time: 41.6 us -> 35.6 us (0.86)
  Pallas kernels: 39.1 us -> 34.1 us
  local copies, waits for them, and re-layouts: 1.67 us -> 0.71 us
    pallas_call x1, Pallas kernels: 39.1 us -> 34.1 us  [local_fused(): pl.pallas_call(fused_kernel, out_shape=jax.ShapeDtypeStruct((seg, project...]
    unnamed x1, local copies, waits for them, and re-layouts: 1.67 us -> 0.71 us
where the time goes in v2:
time: 35.6 us; the launch traced here: 35.5 us
  Pallas kernels  34.1 us (96%)
  local copies, waits for them, and re-layouts  0.71 us (2%)
  between operations  0.66 us (2%)
    pallas_call x1, Pallas kernels, local_fused(): pl.pallas_call(fused_kernel, out_shape=jax.ShapeDtypeStruct((seg, project...  34.1 us

profile of v2, /device:TPU:0, one launch (start us, length us, event | category | flops | bytes accessed | tf_op | source)
XLA Modules:
  0.0 35.5 jit_solution(11820386124414465444)
XLA Ops:
  0.7 34.1 %shard_map.73 = bf16[512,256]{1,0:T(8,128)(2,1)S(1)} custom-call(bf16[512,256]{1,0:T(8,128)(2,1)} %feat_hbm.1, s32[2,256]{1,0:T(2,128)} %bitcast.3, s32[1]{0:T(128)S(6)} %copy.9.count_ref, bf16[256,128,128]{2,1,0:T(8,128)(2,1)} %tiles_ref.1, s32[4,128]{1,0:T(4,128)} %bitcast.4, bf16[512,256]{1,0:T(8,128)(2,1)} %proj_hbm.1, f32[1,256]{1,0:T(1,128)} %bitcast.5), custom_call_target="tpu_custom_call" | custom-call | tf_op jit(solution)/shard_map/pallas_call | solution.py:390
  34.8 0.7 %copy.10 = bf16[512,256]{1,0:T(8,128)(2,1)} copy(bf16[512,256]{1,0:T(8,128)(2,1)S(1)} %shard_map.73) | data formatting | bytes 524288

commit v3 on v2

v3 whole, which is shorter than its diff:
```python
import functools

import jax
import jax.numpy as jnp
from jax import lax
from jax.experimental import pallas as pl
from jax.experimental.pallas import tpu as pltpu
from jax.sharding import PartitionSpec as P

BLK = 32
LANES = 128
CHUNKS = 16
PIECES = (2, 4)
NEAR = (1, 4)
ARRIVALS = 8
X, Y = 3, 5
UNROLL = 8
MERGE_LIMIT = 20 * 1024 * 1024
MESH = pl.DeviceIdType.MESH


def block_terms(running, col_blocks, index_block, tile_block, live_block):
    picked = col_blocks[index_block[:, 1]]
    kept = jnp.where(live_block[:, None, None], tile_block, jnp.zeros_like(tile_block))
    product = jnp.einsum("kij,kjf->kif", kept, picked, preferred_element_type=jnp.float32)
    flattened = product.reshape(product.shape[0], -1)
    return running.at[index_block[:, 0]].add(flattened)


def local_sparse(features, in_degree, tile_index, tile_count, adjacency_tiles, projection, out_bias):
    feat_width = features.shape[1]
    tile_size = adjacency_tiles.shape[1]
    slot_total = adjacency_tiles.shape[0]
    gathered = lax.all_gather(features, "row", axis=0, tiled=True)
    col_blocks = gathered.reshape(gathered.shape[0] // tile_size, tile_size, feat_width)
    row_blocks = features.shape[0] * lax.axis_size("col") // tile_size
    live_count = tile_count[0]
    zeroed = jnp.zeros((row_blocks, tile_size * feat_width), jnp.float32)

    def one_step(running, offset):
        index_block = lax.dynamic_slice_in_dim(tile_index, offset, BLK, 0)
        tile_block = lax.dynamic_slice_in_dim(adjacency_tiles, offset, BLK, 0)
        live_block = offset + jnp.arange(BLK, dtype=jnp.int32) < live_count
        return (block_terms(running, col_blocks, index_block, tile_block, live_block), None)

    summed, _ = lax.scan(one_step, zeroed, jnp.arange(0, slot_total, BLK, dtype=jnp.int32))
    partial_value = summed.reshape(row_blocks * tile_size, feat_width)
    own_sums = lax.psum_scatter(partial_value, "col", scatter_dimension=0, tiled=True)
    neighbour_mean = (own_sums / in_degree[:, None].astype(jnp.float32)).astype(jnp.bfloat16)
    joined = jnp.concatenate([features, neighbour_mean], axis=1)
    mixed = jnp.dot(joined, projection, preferred_element_type=jnp.float32) + out_bias[None, :]
    return jnp.maximum(mixed, 0.0).astype(jnp.bfloat16)


def slot_tables(place_ref, count, table_ref, row_blocks, positions):
    slots = place_ref.shape[1]
    chunks = slots // LANES
    slot_row = lax.broadcasted_iota(jnp.int32, (1, slots), 1)
    spot_row = place_ref[1:2, :] * row_blocks + place_ref[0:1, :]
    spot_row = jnp.where(slot_row < count, spot_row, positions)

    def lane(v, i):
        return v[:, i * LANES:(i + 1) * LANES]

    spot = jnp.concatenate(
        [jnp.transpose(jnp.broadcast_to(lane(spot_row, i), (LANES, LANES))) for i in range(chunks)], axis=0)
    slot = lax.broadcasted_iota(jnp.int32, (slots, LANES), 0)
    before = jnp.zeros((slots, LANES), jnp.float32)
    repeat = jnp.zeros((slots, LANES), jnp.float32)
    for i in range(chunks):
        equal = lane(spot_row, i) == spot
        earlier = lane(slot_row, i) < slot
        first = (lane(spot_row, i) < spot) | (equal & earlier)
        before = before + jnp.where(first, 1.0, 0.0)
        repeat = jnp.maximum(repeat, jnp.where(equal & earlier, 1.0, 0.0))
    rank = jnp.sum(before, axis=1, keepdims=True).astype(jnp.int32)
    keep = jnp.max(repeat, axis=1, keepdims=True)
    for i in range(chunks):
        hit = rank == lax.broadcasted_iota(jnp.int32, (slots, LANES), 1) + i * LANES
        order = jnp.sum(jnp.where(hit, slot, 0), axis=0, keepdims=True)
        again = jnp.sum(jnp.where(hit, keep, 0.0), axis=0, keepdims=True)
        table_ref[i:i + 1, :] = order
        table_ref[chunks + i:chunks + i + 1, :] = again.astype(jnp.int32)
    for i in range(positions // LANES):
        here = lax.broadcasted_iota(jnp.int32, (slots, LANES), 1) + i * LANES
        upto = jnp.sum(jnp.where(spot <= here, 1, 0), axis=0, keepdims=True)
        count_here = jnp.sum(jnp.where(spot == here, 1, 0), axis=0, keepdims=True)
        table_ref[2 * chunks + i:2 * chunks + i + 1, :] = jnp.where(count_here > 0, upto - 1, slots)


def fused_kernel(feat_hbm, place_hbm, count_ref, tiles_ref, degree_hbm, proj_hbm, bias_hbm, out_ref,
                 feat_ref, place_ref, degree_ref, proj_ref, bias_ref,
                 stage, merged, table_v, table, gathered, acc, own, hidden, degree_col,
                 send, send_near, relayed, far, near_in,
                 in_sem, tile_sem, table_sem, sent, ag_recv, relay_sem, far_sem, near_sem):
    seg, width = feat_ref.shape
    slots, tile, _ = stage.shape
    halves = width // LANES
    blocks = seg // tile
    n_row, n_col = gathered.shape[1], 4
    row_blocks = n_col * blocks
    positions = blocks * n_row * row_blocks
    half_rows, quarter = seg // 2, seg // 4
    per = slots // CHUNKS
    r = lax.axis_index("row")
    c = lax.axis_index("col")
    one = c // n_col + 1
    near = c ^ 1
    upper = c < 2
    outer = (c == 0) | (c == 3)
    dests = (jnp.where(upper, 3, 0), jnp.where(upper, 2, 1), near, c)

    inputs = [(feat_hbm, feat_ref), (place_hbm, place_ref),
              (degree_hbm, degree_ref), (proj_hbm, proj_ref), (bias_hbm, bias_ref)]

    def fetch(i):
        return pltpu.make_async_copy(*inputs[i], in_sem.at[i])

    for i in range(2):
        fetch(i).start()

    barrier = pltpu.get_barrier_semaphore()

    def greet(row, col):
        pl.semaphore_signal(barrier, inc=1, device_id=(row, col), device_id_type=MESH)

    for m in (1, X, Y):
        greet(r ^ m, c)
    greet(r, near)
    greet(r, c ^ 2)

    @pl.when(jnp.logical_not(outer))
    def _():
        greet(r, c ^ 3)

    for i in range(CHUNKS):
        part = pl.ds(i * per, per)
        pltpu.make_async_copy(tiles_ref.at[part], stage.at[part], tile_sem).start()
    for i in range(2, len(inputs)):
        fetch(i).start()

    rows_of = [pl.ds(i * quarter, quarter) for i in range(4)]
    first_rows, last_rows = pl.ds(0, half_rows), pl.ds(half_rows, half_rows)
    whole = pl.ds(0, seg)
    FROM_SIB, FROM_1, FROM_2, FROM_3, FROM_FAR, SIB_X, SIB_Y, SIB_D = range(ARRIVALS)
    arriving_rows = (seg, half_rows, half_rows, seg, seg, seg, seg, seg)

    def lanes(h):
        return pl.ds(h * LANES, LANES)

    def gather_start(h, flip, rows, step, arrival):
        owner = r ^ flip
        src = feat_ref.at[rows, lanes(h)] if flip == 0 else gathered.at[h, owner, rows, :]
        pltpu.make_async_remote_copy(
            src_ref=src, dst_ref=gathered.at[h, owner, rows, :],
            send_sem=sent, recv_sem=ag_recv.at[h, arrival],
            device_id=(r ^ step, c), device_id_type=MESH).start()

    def wait_for(h, arrival):
        rows = pl.ds(0, arriving_rows[arrival])
        pltpu.make_async_remote_copy(
            src_ref=gathered.at[h, 0, rows, :], dst_ref=gathered.at[h, 0, rows, :],
            send_sem=sent, recv_sem=ag_recv.at[h, arrival],
            device_id=(r ^ 1, c), device_id_type=MESH).wait_recv()

    def gather_own(h):
        gather_start(h, 0, rows_of[0], X, FROM_1)
        gather_start(h, 0, rows_of[2], Y, FROM_1)
        gather_start(h, 0, whole, 1, FROM_SIB)
        gather_start(h, 0, rows_of[1], X, FROM_2)
        gather_start(h, 0, rows_of[3], Y, FROM_2)
        gather_start(h, 0, last_rows, X, FROM_3)
        gather_start(h, 0, first_rows, Y, FROM_3)

    def forward(h, part):
        wait_for(h, (FROM_1, FROM_2)[part])
        gather_start(h, X, rows_of[part], Y, FROM_FAR)
        gather_start(h, Y, rows_of[2 + part], X, FROM_FAR)

    def share_near(h):
        wait_for(h, FROM_3)
        gather_start(h, X, whole, 1, SIB_X)
        gather_start(h, Y, whole, 1, SIB_Y)

    def share_far(h):
        wait_for(h, FROM_FAR)
        gather_start(h, 6, whole, 1, SIB_D)

    def block_of(h, flip):
        if h is None:
            return jnp.concatenate([block_of(i, flip) for i in range(halves)], axis=1)
        return feat_ref[:, lanes(h)] if flip == 0 else gathered[h, r ^ flip]

    def product(h, flips, dest, group=None):
        columns = []
        for flip in flips:
            base = (r ^ flip) * (blocks * row_blocks)
            line = 2 * (slots // LANES) + base // LANES
            spot = base % LANES + dest * blocks
            columns += [(line, spot + k * row_blocks) for k in range(blocks)]
        picks = range(blocks) if group is None else [group * (blocks // 2) + k for k in range(blocks // 2)]
        left = jnp.concatenate(
            [jnp.concatenate([merged[table[line, spot + b]] for line, spot in columns], axis=1)
             for b in picks], axis=0)
        right = jnp.concatenate([block_of(h, flip) for flip in flips], axis=0)
        return jnp.dot(left, right, preferred_element_type=jnp.float32)

    def half_of(g):
        return pl.ds(pl.multiple_of(g * half_rows, half_rows), half_rows)

    def add_pair(h, flips, low, count):
        @pl.loop(low, low + count)
        def _(i):
            dest = jnp.where(i == 0, dests[0], dests[1])
            if flips[0] == 0:
                acc[h, i] = product(h, flips, dest)
            else:
                acc[h, i] += product(h, flips, dest)

    def piece(q, pieces):
        size = seg // pieces
        return pl.ds(pl.multiple_of(q * size, size), size)

    def sum_copy(src, dst, recv, row, col):
        return pltpu.make_async_remote_copy(
            src_ref=src, dst_ref=dst, send_sem=sent, recv_sem=recv,
            device_id=(row, col), device_id_type=MESH)

    def relay_copy(h, i, q):
        rows = piece(q, PIECES[h])
        return sum_copy(send.at[h, i, rows, :], relayed.at[h, i, rows, :],
                        relay_sem.at[2 * sum(PIECES[:h]) + i * PIECES[h] + q], r, near)

    def far_copy(h, i, q):
        rows = piece(q, PIECES[h])
        return sum_copy(send.at[h, i, rows, :], far.at[h, rows, :],
                        far_sem.at[0 if h == 0 else q + 1], r, dests[i])

    def near_copy(h, q):
        rows = piece(q, NEAR[h])
        return sum_copy(send_near.at[h, rows, :], near_in.at[h, rows, :],
                        near_sem.at[sum(NEAR[:h]) + q], r, near)

    def last_pair(h, i):
        each = PIECES[h] // 2

        @pl.loop(0, 2)
        def _(g):
            rows = half_of(g)
            total = acc[h, i, rows, :] + product(h, (6, 7), dests[i], g)
            acc[h, i, rows, :] = total

            @pl.when(outer)
            def _():
                send[h, i, rows, :] = total.astype(send.dtype)
                for k in range(each):
                    relay_copy(h, i, g * each + k).start()

    def relay_sum(h, i, q):
        @pl.when(jnp.logical_not(outer))
        def _():
            rows = piece(q, PIECES[h])
            relay_copy(h, i, q).wait_recv()
            total = acc[h, i, rows, :] + relayed[h, i, rows, :].astype(jnp.float32)
            send[h, i, rows, :] = total.astype(send.dtype)
            far_copy(h, i, q).start()

    def near_segment(h):
        @pl.loop(0, 2)
        def _(g):
            rows = half_of(g)
            send_near[h, rows, :] = product(h, range(n_row), near, g).astype(send_near.dtype)
        for q in range(NEAR[h]):
            near_copy(h, q).start()

    def own_segment():
        @pl.loop(0, 2)
        def _(g):
            own[half_of(g), :] = product(None, range(n_row), c, g)

    def finish():
        sum_copy(far.at[0], far.at[0], far_sem.at[0], r, near).wait_recv()
        near_copy(0, 0).wait_recv()
        pieces = NEAR[1]
        for q in range(pieces):
            rows = piece(q, pieces)
            far_copy(1, 0, q).wait_recv()
            near_copy(1, q).wait_recv()
            divisor = degree_col[rows, :]
            mean = jnp.concatenate(
                [((own[rows, lanes(h)] + far[h, rows, :].astype(jnp.float32)
                   + near_in[h, rows, :].astype(jnp.float32)) / divisor).astype(jnp.bfloat16)
                 for h in range(halves)], axis=1)
            mixed = hidden[rows, :] + jnp.dot(
                mean, proj_ref[width:, :], preferred_element_type=jnp.float32)
            out_ref[rows, :] = jnp.maximum(mixed, 0.0).astype(out_ref.dtype)

    def tables():
        fetch(1).wait()
        merged[slots] = jnp.zeros((tile, tile), merged.dtype)
        slot_tables(place_ref, count_ref[0], table_v, row_blocks, positions)

    table_copy = pltpu.make_async_copy(table_v, table, table_sem)

    def wait_loads():
        table_copy.wait()
        pltpu.make_async_copy(tiles_ref, stage, tile_sem).wait()

    def merge_slots(low, high, running):
        for part in range(slots // LANES):
            def merge(i, running, part=part):
                keep = table[slots // LANES + part, i].astype(jnp.float32)
                kept = jnp.broadcast_to(keep, (16, tile)).astype(running.dtype)
                kept = jnp.concatenate([kept] * (tile // 16), axis=0)
                running = stage[table[part, i]] + running * kept
                merged[part * LANES + i] = running
                return running
            begin, end = max(low - part * LANES, 0), min(high - part * LANES, LANES)
            if begin < end:
                running = lax.fori_loop(begin, end, merge, running, unroll=UNROLL)
        return running

    def prepare():
        for i in range(2, len(inputs)):
            fetch(i).wait()
        hidden[...] = jnp.dot(
            feat_ref[...], proj_ref[:width, :], preferred_element_type=jnp.float32) + bias_ref[...]
        for b in range(seg // LANES):
            one = degree_ref[b:b + 1, :].astype(jnp.float32)
            degree_col[b * LANES:(b + 1) * LANES, :] = jnp.transpose(jnp.broadcast_to(one, (LANES, LANES)))

    def drain():
        tiles_sent = halves * 10 * seg * LANES // (tile * tile)
        sum_copy(stage.at[pl.ds(0, tiles_sent)], stage.at[pl.ds(0, tiles_sent)],
                 near_sem.at[0], r, near).wait_send()

    def step(name, run, *args):
        with jax.named_scope(name):
            return run(*args)

    early = slots // 4
    step("w_feat", fetch(0).wait)
    step("barrier", pl.semaphore_wait, barrier, jnp.where(outer, 5, 6))
    step("own0", gather_own, 0)
    step("tables", tables)
    table_copy.start()
    step("loads", wait_loads)
    step("forward0a", forward, 0, 0)
    running = step("merge0", merge_slots, 0, early, jnp.zeros((tile, tile), merged.dtype))
    step("forward0b", forward, 0, 1)
    step("own1", gather_own, 1)
    step("merge1", merge_slots, early, slots, running)
    step("w_sib0", wait_for, 0, FROM_SIB)
    step("pair0a0", add_pair, 0, (0, 1), 0, one)
    step("share_near0", share_near, 0)
    step("pair0a1", add_pair, 0, (0, 1), 1, one)
    step("share_far0", share_far, 0)
    step("w_x0", wait_for, 0, SIB_X)
    step("pair0x0", add_pair, 0, (2, 3), 0, one)
    step("w_y0", wait_for, 0, SIB_Y)
    step("pair0y0", add_pair, 0, (4, 5), 0, one)
    step("w_d0", wait_for, 0, SIB_D)
    step("last00", last_pair, 0, 0)
    step("forward1a", forward, 1, 0)
    step("pair0x1", add_pair, 0, (2, 3), 1, one)
    step("forward1b", forward, 1, 1)
    step("pair0y1", add_pair, 0, (4, 5), 1, one)
    step("last01", last_pair, 0, 1)
    step("near_seg0", near_segment, 0)
    step("w_sib1", wait_for, 1, FROM_SIB)
    step("pair1a", add_pair, 1, (0, 1), 0, 2)
    step("share_near1", share_near, 1)
    step("w_x1", wait_for, 1, SIB_X)
    step("pair1x", add_pair, 1, (2, 3), 0, 2)
    step("share_far1", share_far, 1)
    step("w_y1", wait_for, 1, SIB_Y)
    step("pair1y", add_pair, 1, (4, 5), 0, 2)
    step("relay000", relay_sum, 0, 0, 0)
    step("w_d1", wait_for, 1, SIB_D)
    step("last10", last_pair, 1, 0)
    step("last11", last_pair, 1, 1)
    step("relay001", relay_sum, 0, 0, 1)
    step("relay010", relay_sum, 0, 1, 0)
    step("near_seg1", near_segment, 1)
    step("relay011", relay_sum, 0, 1, 1)
    step("own_seg", own_segment)
    step("prepare", prepare)
    for i in range(2):
        for q in range(PIECES[1]):
            step("relay1", relay_sum, 1, i, q)
    step("finish", finish)
    step("drain", drain)


def local_fused(n_row, n_col, features, in_degree, tile_index, tile_count, adjacency_tiles, projection, out_bias):
    seg, width = features.shape
    slots, tile, _ = adjacency_tiles.shape
    halves = width // LANES
    positions = (seg * n_col // tile) * (seg * n_row // tile)
    lines = 2 * (slots // LANES) + positions // LANES
    hbm = pl.BlockSpec(memory_space=pltpu.HBM)
    args = [features, tile_index.T, tile_count, adjacency_tiles,
            in_degree.reshape(seg // LANES, LANES), projection, out_bias[None, :]]
    specs = [hbm] * len(args)
    specs[2] = pl.BlockSpec(memory_space=pltpu.SMEM)
    args = [a if i == 2 else pltpu.with_memory_space_constraint(a, pltpu.HBM) for i, a in enumerate(args)]
    return pl.pallas_call(
        fused_kernel,
        out_shape=jax.ShapeDtypeStruct((seg, projection.shape[1]), jnp.bfloat16),
        in_specs=specs,
        out_specs=pl.BlockSpec(memory_space=pltpu.VMEM),
        scratch_shapes=[
            pltpu.VMEM(features.shape, features.dtype),
            pltpu.VMEM((2, slots), jnp.int32),
            pltpu.VMEM((seg // LANES, LANES), jnp.int32),
            pltpu.VMEM(projection.shape, projection.dtype),
            pltpu.VMEM((1, projection.shape[1]), jnp.float32),
            pltpu.VMEM((slots, tile, tile), jnp.bfloat16),
            pltpu.VMEM((slots + 1, tile, tile), jnp.bfloat16),
            pltpu.VMEM((lines, LANES), jnp.int32),
            pltpu.SMEM((lines, LANES), jnp.int32),
            pltpu.VMEM((halves, n_row, seg, LANES), jnp.bfloat16),
            pltpu.VMEM((halves, 2, seg, LANES), jnp.float32),
            pltpu.VMEM((seg, width), jnp.float32),
            pltpu.VMEM((seg, projection.shape[1]), jnp.float32),
            pltpu.VMEM((seg, LANES), jnp.float32),
            pltpu.VMEM((halves, 2, seg, LANES), jnp.bfloat16),
            pltpu.VMEM((halves, seg, LANES), jnp.bfloat16),
            pltpu.VMEM((halves, 2, seg, LANES), jnp.bfloat16),
            pltpu.VMEM((halves, seg, LANES), jnp.bfloat16),
            pltpu.VMEM((halves, seg, LANES), jnp.bfloat16),
            pltpu.SemaphoreType.DMA((len(args) - 2,)),
            pltpu.SemaphoreType.DMA,
            pltpu.SemaphoreType.DMA,
            pltpu.SemaphoreType.DMA,
            pltpu.SemaphoreType.DMA((halves, ARRIVALS)),
            pltpu.SemaphoreType.DMA((2 * sum(PIECES),)),
            pltpu.SemaphoreType.DMA((1 + PIECES[1],)),
            pltpu.SemaphoreType.DMA((sum(NEAR),)),
        ],
        compiler_params=pltpu.CompilerParams(
            collective_id=0, has_side_effects=True, vmem_limit_bytes=48 * 1024 * 1024),
    )(*args)


def solution(mesh):
    n_row, n_col = mesh.shape["row"], mesh.shape["col"]

    def local(features, in_degree, tile_index, tile_count, adjacency_tiles, projection, out_bias):
        seg, width = features.shape
        slots, tile, _ = adjacency_tiles.shape
        positions = (seg * n_col // LANES) * (seg * n_row // LANES)
        fits = (
            n_row == 8 and n_col == 4 and tile == LANES and slots <= 256 and slots % LANES == 0
            and 4 * slots * tile * tile <= MERGE_LIMIT
            and seg % (4 * LANES) == 0 and width == 2 * LANES and positions % LANES == 0
            and LANES % (positions // n_row) == 0)
        args = (features, in_degree, tile_index, tile_count, adjacency_tiles, projection, out_bias)
        return local_fused(n_row, n_col, *args) if fits else local_sparse(*args)

    return jax.shard_map(
        local,
        mesh=mesh,
        in_specs=(
            P(("row", "col"), None),
            P(("row", "col")),
            P(("row", "col"), None),
            P(("row", "col")),
            P(("row", "col"), None, None),
            P(),
            P(),
        ),
        out_specs=P(("row", "col"), None),
        check_vma=False,
    )
```

time: 35.6 us -> 33.6 us (0.944)
  Pallas kernels: 34.1 us -> 32 us
    pallas_call x1, Pallas kernels: 34.1 us -> 32 us  [local_fused(): pl.pallas_call(fused_kernel, out_shape=jax.ShapeDtypeStruct((seg, project...]
where the time goes in v3:
time: 33.6 us; the launch traced here: 33.3 us
  Pallas kernels  32 us (95%)
  local copies, waits for them, and re-layouts  0.71 us (2%)
  between operations  0.66 us (2%)
    pallas_call x1, Pallas kernels, local_fused(): pl.pallas_call(fused_kernel, out_shape=jax.ShapeDtypeStruct((seg, project...  32 us
    unnamed x1, local copies, waits for them, and re-layouts  0.71 us

profile of v3, /device:TPU:0, one launch (start us, length us, event | category | flops | bytes accessed | tf_op | source)
XLA Modules:
  0.0 33.3 jit_solution(2321139999747689134)
XLA Ops:
  0.7 32.0 %shard_map.73 = bf16[512,256]{1,0:T(8,128)(2,1)S(1)} custom-call(bf16[512,256]{1,0:T(8,128)(2,1)} %feat_hbm.1, s32[2,256]{1,0:T(2,128)} %bitcast.3, s32[1]{0:T(128)S(6)} %copy.9.count_ref, bf16[256,128,128]{2,1,0:T(8,128)(2,1)} %tiles_ref.1, s32[4,128]{1,0:T(4,128)} %bitcast.4, bf16[512,256]{1,0:T(8,128)(2,1)} %proj_hbm.1, f32[1,256]{1,0:T(1,128)} %bitcast.5), custom_call_target="tpu_custom_call" | custom-call | tf_op jit(solution)/shard_map/pallas_call | solution.py:407
  32.6 0.7 %copy.10 = bf16[512,256]{1,0:T(8,128)(2,1)} copy(bf16[512,256]{1,0:T(8,128)(2,1)S(1)} %shard_map.73) | data formatting | bytes 524288

commit v4 on v3

--- a/solution.py
+++ b/solution.py
@@ -11,8 +11,8 @@
 LANES = 128
 CHUNKS = 16
 PIECES = (2, 4)
-NEAR = (1, 4)
-ARRIVALS = 8
+NEAR = (2, 4)
+ARRIVALS = 6
 X, Y = 3, 5
 UNROLL = 8
 MERGE_LIMIT = 20 * 1024 * 1024
@@ -133,17 +133,17 @@
     def _():
         greet(r, c ^ 3)
 
+    for i in range(2, len(inputs)):
+        fetch(i).start()
     for i in range(CHUNKS):
         part = pl.ds(i * per, per)
         pltpu.make_async_copy(tiles_ref.at[part], stage.at[part], tile_sem).start()
-    for i in range(2, len(inputs)):
-        fetch(i).start()
 
     rows_of = [pl.ds(i * quarter, quarter) for i in range(4)]
     first_rows, last_rows = pl.ds(0, half_rows), pl.ds(half_rows, half_rows)
     whole = pl.ds(0, seg)
-    FROM_SIB, FROM_1, FROM_2, FROM_3, FROM_FAR, SIB_X, SIB_Y, SIB_D = range(ARRIVALS)
-    arriving_rows = (seg, half_rows, half_rows, seg, seg, seg, seg, seg)
+    FROM_1, FROM_2, FROM_3, FROM_FAR, SIB_XY, SIB_D = range(ARRIVALS)
+    arriving_rows = (half_rows, half_rows, 2 * seg, seg, 2 * seg, seg)
 
     def lanes(h):
         return pl.ds(h * LANES, LANES)
@@ -157,16 +157,20 @@
             device_id=(r ^ step, c), device_id_type=MESH).start()
 
     def wait_for(h, arrival):
-        rows = pl.ds(0, arriving_rows[arrival])
+        rows = arriving_rows[arrival]
+        if rows <= seg:
+            ref = gathered.at[h, 0, pl.ds(0, rows), :]
+        else:
+            ref = gathered.at[h, pl.ds(0, rows // seg)]
         pltpu.make_async_remote_copy(
-            src_ref=gathered.at[h, 0, rows, :], dst_ref=gathered.at[h, 0, rows, :],
+            src_ref=ref, dst_ref=ref,
             send_sem=sent, recv_sem=ag_recv.at[h, arrival],
             device_id=(r ^ 1, c), device_id_type=MESH).wait_recv()
 
     def gather_own(h):
         gather_start(h, 0, rows_of[0], X, FROM_1)
         gather_start(h, 0, rows_of[2], Y, FROM_1)
-        gather_start(h, 0, whole, 1, FROM_SIB)
+        gather_start(h, 0, whole, 1, FROM_3)
         gather_start(h, 0, rows_of[1], X, FROM_2)
         gather_start(h, 0, rows_of[3], Y, FROM_2)
         gather_start(h, 0, last_rows, X, FROM_3)
@@ -179,8 +183,8 @@
 
     def share_near(h):
         wait_for(h, FROM_3)
-        gather_start(h, X, whole, 1, SIB_X)
-        gather_start(h, Y, whole, 1, SIB_Y)
+        gather_start(h, X, whole, 1, SIB_XY)
+        gather_start(h, Y, whole, 1, SIB_XY)
 
     def share_far(h):
         wait_for(h, FROM_FAR)
@@ -239,7 +243,7 @@
     def near_copy(h, q):
         rows = piece(q, NEAR[h])
         return sum_copy(send_near.at[h, rows, :], near_in.at[h, rows, :],
-                        near_sem.at[sum(NEAR[:h]) + q], r, near)
+                        near_sem.at[0 if h == 0 else q + 1], r, near)
 
     def last_pair(h, i):
         each = PIECES[h] // 2
@@ -265,13 +269,32 @@
             send[h, i, rows, :] = total.astype(send.dtype)
             far_copy(h, i, q).start()
 
-    def near_segment(h):
-        @pl.loop(0, 2)
+    def near_product(h, trips):
+        @pl.loop(0, trips)
         def _(g):
             rows = half_of(g)
             send_near[h, rows, :] = product(h, range(n_row), near, g).astype(send_near.dtype)
-        for q in range(NEAR[h]):
-            near_copy(h, q).start()
+
+    def near_segment(mine):
+        near_product(1, jnp.where(mine, 2, 0))
+
+        @pl.when(mine)
+        def _():
+            for q in range(NEAR[1]):
+                near_copy(1, q).start()
+
+    def near_first():
+        near_product(0, 2)
+        near_copy(0, 0).start()
+
+        @pl.when(jnp.logical_not(outer))
+        def _():
+            near_copy(0, 1).start()
+
+    def near_rest():
+        @pl.when(outer)
+        def _():
+            near_copy(0, 1).start()
 
     def own_segment():
         @pl.loop(0, 2)
@@ -280,7 +303,7 @@
 
     def finish():
         sum_copy(far.at[0], far.at[0], far_sem.at[0], r, near).wait_recv()
-        near_copy(0, 0).wait_recv()
+        sum_copy(near_in.at[0], near_in.at[0], near_sem.at[0], r, near).wait_recv()
         pieces = NEAR[1]
         for q in range(pieces):
             rows = piece(q, pieces)
@@ -344,20 +367,19 @@
     step("own0", gather_own, 0)
     step("tables", tables)
     table_copy.start()
+    step("prepare", prepare)
     step("loads", wait_loads)
     step("forward0a", forward, 0, 0)
     running = step("merge0", merge_slots, 0, early, jnp.zeros((tile, tile), merged.dtype))
     step("forward0b", forward, 0, 1)
     step("own1", gather_own, 1)
     step("merge1", merge_slots, early, slots, running)
-    step("w_sib0", wait_for, 0, FROM_SIB)
+    step("share_near0", share_near, 0)
     step("pair0a0", add_pair, 0, (0, 1), 0, one)
-    step("share_near0", share_near, 0)
     step("pair0a1", add_pair, 0, (0, 1), 1, one)
     step("share_far0", share_far, 0)
-    step("w_x0", wait_for, 0, SIB_X)
+    step("w_x0", wait_for, 0, SIB_XY)
     step("pair0x0", add_pair, 0, (2, 3), 0, one)
-    step("w_y0", wait_for, 0, SIB_Y)
     step("pair0y0", add_pair, 0, (4, 5), 0, one)
     step("w_d0", wait_for, 0, SIB_D)
     step("last00", last_pair, 0, 0)
@@ -366,28 +388,27 @@
     step("forward1b", forward, 1, 1)
     step("pair0y1", add_pair, 0, (4, 5), 1, one)
     step("last01", last_pair, 0, 1)
-    step("near_seg0", near_segment, 0)
-    step("w_sib1", wait_for, 1, FROM_SIB)
+    step("share_near1", share_near, 1)
+    step("near_seg0", near_first)
+    step("relay000", relay_sum, 0, 0, 0)
     step("pair1a", add_pair, 1, (0, 1), 0, 2)
-    step("share_near1", share_near, 1)
-    step("w_x1", wait_for, 1, SIB_X)
+    step("share_far1", share_far, 1)
+    step("w_x1", wait_for, 1, SIB_XY)
     step("pair1x", add_pair, 1, (2, 3), 0, 2)
-    step("share_far1", share_far, 1)
-    step("w_y1", wait_for, 1, SIB_Y)
+    step("relay001", relay_sum, 0, 0, 1)
     step("pair1y", add_pair, 1, (4, 5), 0, 2)
-    step("relay000", relay_sum, 0, 0, 0)
+    step("relay010", relay_sum, 0, 1, 0)
     step("w_d1", wait_for, 1, SIB_D)
+    step("near_seg1i", near_segment, jnp.logical_not(outer))
+    step("relay011", relay_sum, 0, 1, 1)
     step("last10", last_pair, 1, 0)
     step("last11", last_pair, 1, 1)
-    step("relay001", relay_sum, 0, 0, 1)
-    step("relay010", relay_sum, 0, 1, 0)
-    step("near_seg1", near_segment, 1)
-    step("relay011", relay_sum, 0, 1, 1)
-    step("own_seg", own_segment)
-    step("prepare", prepare)
+    near_rest()
+    step("near_seg1o", near_segment, outer)
     for i in range(2):
         for q in range(PIECES[1]):
-            step("relay1", relay_sum, 1, i, q)
+            step(f"relay1{i}{q}", relay_sum, 1, i, q)
+    step("own_seg", own_segment)
     step("finish", finish)
     step("drain", drain)
 
@@ -436,7 +457,7 @@
             pltpu.SemaphoreType.DMA((halves, ARRIVALS)),
             pltpu.SemaphoreType.DMA((2 * sum(PIECES),)),
             pltpu.SemaphoreType.DMA((1 + PIECES[1],)),
-            pltpu.SemaphoreType.DMA((sum(NEAR),)),
+            pltpu.SemaphoreType.DMA((1 + NEAR[1],)),
         ],
         compiler_params=pltpu.CompilerParams(
             collective_id=0, has_side_effects=True, vmem_limit_bytes=48 * 1024 * 1024),

time: 33.6 us -> 32.4 us (0.964)
  Pallas kernels: 32 us -> 30.9 us
    pallas_call x1, Pallas kernels: 32 us -> 30.9 us  [local_fused(): pl.pallas_call(fused_kernel, out_shape=jax.ShapeDtypeStruct((seg, project...]
where the time goes in v4:
time: 32.4 us; the launch traced here: 32.2 us
  Pallas kernels  30.9 us (95%)
  local copies, waits for them, and re-layouts  0.71 us (2%)
  between operations  0.66 us (2%)
    pallas_call x1, Pallas kernels, local_fused(): pl.pallas_call(fused_kernel, out_shape=jax.ShapeDtypeStruct((seg, project...  30.9 us
    unnamed x1, local copies, waits for them, and re-layouts  0.71 us

profile of v4, /device:TPU:0, one launch (start us, length us, event | category | flops | bytes accessed | tf_op | source)
XLA Modules:
  0.0 32.2 jit_solution(13324042016708756900)
XLA Ops:
  0.7 30.9 %shard_map.73 = bf16[512,256]{1,0:T(8,128)(2,1)S(1)} custom-call(bf16[512,256]{1,0:T(8,128)(2,1)} %feat_hbm.1, s32[2,256]{1,0:T(2,128)} %bitcast.3, s32[1]{0:T(128)S(6)} %copy.9.count_ref, bf16[256,128,128]{2,1,0:T(8,128)(2,1)} %tiles_ref.1, s32[4,128]{1,0:T(4,128)} %bitcast.4, bf16[512,256]{1,0:T(8,128)(2,1)} %proj_hbm.1, f32[1,256]{1,0:T(1,128)} %bitcast.5), custom_call_target="tpu_custom_call" | custom-call | tf_op jit(solution)/shard_map/pallas_call | solution.py:428
  31.5 0.7 %copy.10 = bf16[512,256]{1,0:T(8,128)(2,1)} copy(bf16[512,256]{1,0:T(8,128)(2,1)S(1)} %shard_map.73) | data formatting | bytes 524288

commit v5 on v4

--- a/solution.py
+++ b/solution.py
@@ -92,7 +92,7 @@
                  feat_ref, place_ref, degree_ref, proj_ref, bias_ref,
                  stage, merged, table_v, table, gathered, acc, own, hidden, degree_col,
                  send, send_near, relayed, far, near_in,
-                 in_sem, tile_sem, table_sem, sent, ag_recv, relay_sem, far_sem, near_sem):
+                 in_sem, tile_sem, table_sem, sent, ag_recv, relay_sem, far_sem, near_sem, inner_ready):
     seg, width = feat_ref.shape
     slots, tile, _ = stage.shape
     halves = width // LANES
@@ -110,14 +110,24 @@
     outer = (c == 0) | (c == 3)
     dests = (jnp.where(upper, 3, 0), jnp.where(upper, 2, 1), near, c)
 
-    inputs = [(feat_hbm, feat_ref), (place_hbm, place_ref),
-              (degree_hbm, degree_ref), (proj_hbm, proj_ref), (bias_hbm, bias_ref)]
+    inputs = [(place_hbm, place_ref), (degree_hbm, degree_ref), (proj_hbm, proj_ref), (bias_hbm, bias_ref)]
+
+    def lanes(h):
+        return pl.ds(h * LANES, LANES)
 
     def fetch(i):
-        return pltpu.make_async_copy(*inputs[i], in_sem.at[i])
-
-    for i in range(2):
-        fetch(i).start()
+        return pltpu.make_async_copy(*inputs[i], in_sem.at[halves + i])
+
+    def fetch_features(h, rows):
+        return pltpu.make_async_copy(feat_hbm.at[rows, lanes(h)], feat_ref.at[rows, lanes(h)], in_sem.at[h])
+
+    rows_of = [pl.ds(i * quarter, quarter) for i in range(4)]
+    whole = pl.ds(0, seg)
+    for rows in rows_of:
+        fetch_features(0, rows).start()
+    fetch(0).start()
+    for h in range(1, halves):
+        fetch_features(h, whole).start()
 
     barrier = pltpu.get_barrier_semaphore()
 
@@ -126,27 +136,25 @@
 
     for m in (1, X, Y):
         greet(r ^ m, c)
-    greet(r, near)
-    greet(r, c ^ 2)
+
+    @pl.when(outer)
+    def _():
+        greet(r, near)
+        greet(r, c ^ 2)
 
     @pl.when(jnp.logical_not(outer))
     def _():
         greet(r, c ^ 3)
 
-    for i in range(2, len(inputs)):
+    for i in range(1, len(inputs)):
         fetch(i).start()
     for i in range(CHUNKS):
         part = pl.ds(i * per, per)
         pltpu.make_async_copy(tiles_ref.at[part], stage.at[part], tile_sem).start()
 
-    rows_of = [pl.ds(i * quarter, quarter) for i in range(4)]
     first_rows, last_rows = pl.ds(0, half_rows), pl.ds(half_rows, half_rows)
-    whole = pl.ds(0, seg)
     FROM_1, FROM_2, FROM_3, FROM_FAR, SIB_XY, SIB_D = range(ARRIVALS)
     arriving_rows = (half_rows, half_rows, 2 * seg, seg, 2 * seg, seg)
-
-    def lanes(h):
-        return pl.ds(h * LANES, LANES)
 
     def gather_start(h, flip, rows, step, arrival):
         owner = r ^ flip
@@ -170,11 +178,13 @@
     def gather_own(h):
         gather_start(h, 0, rows_of[0], X, FROM_1)
         gather_start(h, 0, rows_of[2], Y, FROM_1)
-        gather_start(h, 0, whole, 1, FROM_3)
         gather_start(h, 0, rows_of[1], X, FROM_2)
         gather_start(h, 0, rows_of[3], Y, FROM_2)
         gather_start(h, 0, last_rows, X, FROM_3)
         gather_start(h, 0, first_rows, Y, FROM_3)
+
+    def gather_sibling(h):
+        gather_start(h, 0, whole, 1, FROM_3)
 
     def forward(h, part):
         wait_for(h, (FROM_1, FROM_2)[part])
@@ -268,6 +278,17 @@
             total = acc[h, i, rows, :] + relayed[h, i, rows, :].astype(jnp.float32)
             send[h, i, rows, :] = total.astype(send.dtype)
             far_copy(h, i, q).start()
+
+    def tell_outer():
+        @pl.when(jnp.logical_not(outer))
+        def _():
+            for col in (near, c ^ 2):
+                pl.semaphore_signal(inner_ready, inc=1, device_id=(r, col), device_id_type=MESH)
+
+    def hear_inner():
+        @pl.when(outer)
+        def _():
+            pl.semaphore_wait(inner_ready, 2)
 
     def near_product(h, trips):
         @pl.loop(0, trips)
@@ -319,7 +340,7 @@
             out_ref[rows, :] = jnp.maximum(mixed, 0.0).astype(out_ref.dtype)
 
     def tables():
-        fetch(1).wait()
+        fetch(0).wait()
         merged[slots] = jnp.zeros((tile, tile), merged.dtype)
         slot_tables(place_ref, count_ref[0], table_v, row_blocks, positions)
 
@@ -344,7 +365,9 @@
         return running
 
     def prepare():
-        for i in range(2, len(inputs)):
+        for h in range(1, halves):
+            fetch_features(h, whole).wait()
+        for i in range(1, len(inputs)):
             fetch(i).wait()
         hidden[...] = jnp.dot(
             feat_ref[...], proj_ref[:width, :], preferred_element_type=jnp.float32) + bias_ref[...]
@@ -362,9 +385,11 @@
             return run(*args)
 
     early = slots // 4
-    step("w_feat", fetch(0).wait)
-    step("barrier", pl.semaphore_wait, barrier, jnp.where(outer, 5, 6))
+    step("w_feat", fetch_features(0, whole).wait)
+    step("barrier", pl.semaphore_wait, barrier, jnp.where(outer, 3, 6))
     step("own0", gather_own, 0)
+    gather_sibling(0)
+    tell_outer()
     step("tables", tables)
     table_copy.start()
     step("prepare", prepare)
@@ -372,29 +397,31 @@
     step("forward0a", forward, 0, 0)
     running = step("merge0", merge_slots, 0, early, jnp.zeros((tile, tile), merged.dtype))
     step("forward0b", forward, 0, 1)
-    step("own1", gather_own, 1)
     step("merge1", merge_slots, early, slots, running)
     step("share_near0", share_near, 0)
     step("pair0a0", add_pair, 0, (0, 1), 0, one)
     step("pair0a1", add_pair, 0, (0, 1), 1, one)
     step("share_far0", share_far, 0)
+    step("own1", gather_own, 1)
+    gather_sibling(1)
     step("w_x0", wait_for, 0, SIB_XY)
     step("pair0x0", add_pair, 0, (2, 3), 0, one)
     step("pair0y0", add_pair, 0, (4, 5), 0, one)
     step("w_d0", wait_for, 0, SIB_D)
+    hear_inner()
     step("last00", last_pair, 0, 0)
-    step("forward1a", forward, 1, 0)
     step("pair0x1", add_pair, 0, (2, 3), 1, one)
-    step("forward1b", forward, 1, 1)
     step("pair0y1", add_pair, 0, (4, 5), 1, one)
     step("last01", last_pair, 0, 1)
+    step("forward1a", forward, 1, 0)
+    step("forward1b", forward, 1, 1)
+    step("near_seg0", near_first)
     step("share_near1", share_near, 1)
-    step("near_seg0", near_first)
     step("relay000", relay_sum, 0, 0, 0)
     step("pair1a", add_pair, 1, (0, 1), 0, 2)
-    step("share_far1", share_far, 1)
     step("w_x1", wait_for, 1, SIB_XY)
     step("pair1x", add_pair, 1, (2, 3), 0, 2)
+    step("share_far1", share_far, 1)
     step("relay001", relay_sum, 0, 0, 1)
     step("pair1y", add_pair, 1, (4, 5), 0, 2)
     step("relay010", relay_sum, 0, 1, 0)
@@ -450,7 +477,7 @@
             pltpu.VMEM((halves, 2, seg, LANES), jnp.bfloat16),
             pltpu.VMEM((halves, seg, LANES), jnp.bfloat16),
             pltpu.VMEM((halves, seg, LANES), jnp.bfloat16),
-            pltpu.SemaphoreType.DMA((len(args) - 2,)),
+            pltpu.SemaphoreType.DMA((halves + len(args) - 3,)),
             pltpu.SemaphoreType.DMA,
             pltpu.SemaphoreType.DMA,
             pltpu.SemaphoreType.DMA,
@@ -458,6 +485,7 @@
             pltpu.SemaphoreType.DMA((2 * sum(PIECES),)),
             pltpu.SemaphoreType.DMA((1 + PIECES[1],)),
             pltpu.SemaphoreType.DMA((1 + NEAR[1],)),
+            pltpu.SemaphoreType.REGULAR,
         ],
         compiler_params=pltpu.CompilerParams(
             collective_id=0, has_side_effects=True, vmem_limit_bytes=48 * 1024 * 1024),

time: 32.4 us -> 31.7 us (0.978)
  Pallas kernels: 30.9 us -> 30.2 us
    pallas_call x1, Pallas kernels: 30.9 us -> 30.2 us  [local_fused(): pl.pallas_call(fused_kernel, out_shape=jax.ShapeDtypeStruct((seg, project...]
where the time goes in v5:
time: 31.7 us; the launch traced here: 31.6 us
  Pallas kernels  30.2 us (95%)
  local copies, waits for them, and re-layouts  0.71 us (2%)
  between operations  0.66 us (2%)
    pallas_call x1, Pallas kernels, local_fused(): pl.pallas_call(fused_kernel, out_shape=jax.ShapeDtypeStruct((seg, project...  30.2 us
    unnamed x1, local copies, waits for them, and re-layouts  0.71 us

profile of v5, /device:TPU:0, one launch (start us, length us, event | category | flops | bytes accessed | tf_op | source)
XLA Modules:
  0.0 31.6 jit_solution(8412567655841457676)
XLA Ops:
  0.7 30.2 %shard_map.73 = bf16[512,256]{1,0:T(8,128)(2,1)S(1)} custom-call(bf16[512,256]{1,0:T(8,128)(2,1)} %feat_hbm.1, s32[2,256]{1,0:T(2,128)} %bitcast.3, s32[1]{0:T(128)S(6)} %copy.9.count_ref, bf16[256,128,128]{2,1,0:T(8,128)(2,1)} %tiles_ref.1, s32[4,128]{1,0:T(4,128)} %bitcast.4, bf16[512,256]{1,0:T(8,128)(2,1)} %proj_hbm.1, f32[1,256]{1,0:T(1,128)} %bitcast.5), custom_call_target="tpu_custom_call" | custom-call | tf_op jit(solution)/shard_map/pallas_call | solution.py:455
  30.9 0.7 %copy.10 = bf16[512,256]{1,0:T(8,128)(2,1)} copy(bf16[512,256]{1,0:T(8,128)(2,1)S(1)} %shard_map.73) | data formatting | bytes 524288

commit v6 on v5

--- a/solution.py
+++ b/solution.py
@@ -304,13 +304,25 @@
             for q in range(NEAR[1]):
                 near_copy(1, q).start()
 
-    def near_first():
-        near_product(0, 2)
-        near_copy(0, 0).start()
-
-        @pl.when(jnp.logical_not(outer))
-        def _():
-            near_copy(0, 1).start()
+    def near_first(mine, pieces):
+        near_product(0, jnp.where(mine, 2, 0))
+
+        @pl.when(mine)
+        def _():
+            for q in range(pieces):
+                near_copy(0, q).start()
+
+    def when(mine, *runs):
+        @pl.when(mine)
+        def _():
+            for run, *args in runs:
+                run(*args)
+
+    def forwards(mine):
+        @pl.when(mine)
+        def _():
+            forward(1, 0)
+            forward(1, 1)
 
     def near_rest():
         @pl.when(outer)
@@ -385,6 +397,7 @@
             return run(*args)
 
     early = slots // 4
+    inner = jnp.logical_not(outer)
     step("w_feat", fetch_features(0, whole).wait)
     step("barrier", pl.semaphore_wait, barrier, jnp.where(outer, 3, 6))
     step("own0", gather_own, 0)
@@ -397,26 +410,29 @@
     step("forward0a", forward, 0, 0)
     running = step("merge0", merge_slots, 0, early, jnp.zeros((tile, tile), merged.dtype))
     step("forward0b", forward, 0, 1)
+    step("own1i", when, inner, (gather_own, 1), (gather_sibling, 1))
     step("merge1", merge_slots, early, slots, running)
     step("share_near0", share_near, 0)
     step("pair0a0", add_pair, 0, (0, 1), 0, one)
     step("pair0a1", add_pair, 0, (0, 1), 1, one)
     step("share_far0", share_far, 0)
-    step("own1", gather_own, 1)
-    gather_sibling(1)
+    step("own1o", when, outer, (gather_own, 1))
     step("w_x0", wait_for, 0, SIB_XY)
     step("pair0x0", add_pair, 0, (2, 3), 0, one)
     step("pair0y0", add_pair, 0, (4, 5), 0, one)
     step("w_d0", wait_for, 0, SIB_D)
+    step("near_seg0i", near_first, inner, NEAR[0])
+    step("forward1i", forwards, inner)
+    step("share_near1i", when, inner, (share_near, 1))
     hear_inner()
     step("last00", last_pair, 0, 0)
+    when(outer, (gather_sibling, 1))
     step("pair0x1", add_pair, 0, (2, 3), 1, one)
     step("pair0y1", add_pair, 0, (4, 5), 1, one)
     step("last01", last_pair, 0, 1)
-    step("forward1a", forward, 1, 0)
-    step("forward1b", forward, 1, 1)
-    step("near_seg0", near_first)
-    step("share_near1", share_near, 1)
+    step("forward1o", forwards, outer)
+    step("near_seg0o", near_first, outer, 1)
+    step("share_near1o", when, outer, (share_near, 1))
     step("relay000", relay_sum, 0, 0, 0)
     step("pair1a", add_pair, 1, (0, 1), 0, 2)
     step("w_x1", wait_for, 1, SIB_XY)

time: 31.7 us -> 31.4 us (level)
  the two profiles are of different devices: /device:TPU:0 before, /device:TPU:17 now
where the time goes in v6:
time: 31.4 us; the launch traced here: 31.2 us
  Pallas kernels  29.9 us (95%)
  local copies, waits for them, and re-layouts  0.71 us (2%)
  between operations  0.66 us (2%)
    pallas_call x1, Pallas kernels, local_fused(): pl.pallas_call(fused_kernel, out_shape=jax.ShapeDtypeStruct((seg, project...  29.9 us
    unnamed x1, local copies, waits for them, and re-layouts  0.71 us

profile of v6, /device:TPU:17, one launch (start us, length us, event | category | flops | bytes accessed | tf_op | source)
XLA Modules:
  0.0 31.2 jit_solution(17741892580200475511)
XLA Ops:
  0.7 29.9 %shard_map.73 = bf16[512,256]{1,0:T(8,128)(2,1)S(1)} custom-call(bf16[512,256]{1,0:T(8,128)(2,1)} %feat_hbm.1, s32[2,256]{1,0:T(2,128)} %bitcast.3, s32[1]{0:T(128)S(6)} %copy.9.count_ref, bf16[256,128,128]{2,1,0:T(8,128)(2,1)} %tiles_ref.1, s32[4,128]{1,0:T(4,128)} %bitcast.4, bf16[512,256]{1,0:T(8,128)(2,1)} %proj_hbm.1, f32[1,256]{1,0:T(1,128)} %bitcast.5), custom_call_target="tpu_custom_call" | custom-call | tf_op jit(solution)/shard_map/pallas_call | solution.py:471
  30.5 0.7 %copy.10 = bf16[512,256]{1,0:T(8,128)(2,1)} copy(bf16[512,256]{1,0:T(8,128)(2,1)S(1)} %shard_map.73) | data formatting | bytes 524288
